TPU v7x, 256 devices: a 4x2x16 block of a 4x16x16 slice. The times are simulated.
256 devices in a mesh: slides: 2 (over y), row: 128 (over x, z, core).
Axes of the slice: x: 4, y: 2, z: 16, core: 2. Of those that a mesh axis runs over, the one named last changes fastest.
The devices are a block of a 4x16x16 slice.
Arguments:
- slide_pixels: bfloat16 [16384, 16384], P(('slides', 'row')), parts along dimension 0, may hold values from -6 to 6
- tissue_mask: int32 [512, 8], P(('slides', 'row')), parts along dimension 0, may hold values from 0 to 1, as said below
- conv_weight: bfloat16 [3, 3, 64, 64], replicated, may hold values from -0.25 to 0.25
- conv_bias: bfloat16 [64], replicated, may hold values from -3 to 3
Outputs:
- packed_tiles: bfloat16 [2048, 32, 2048], P(('slides', 'row')), parts along dimension 0
There are 2 independent parts, one for each index of `slides`. A program takes and returns all parts, laid end to end along the dimension named above; an argument that names none is the same for every part. Nothing has to cross between parts.
Inputs may be any that keep to these rules, and one draw needn't show every extreme that they name: `tissue_mask`: exactly 1024 tiles hold tissue. For every s from 1 to 127, the first s * 2 tile rows hold s * 8 + e tissue tiles with e between 0 and 2; e = 2 occurs in every draw. For every such s, some column holds tissue in both tile row s * 2 - 1 and tile row s * 2.
All inputs are finite; a program needn't handle non-finite values.
Results may differ from a plain program's by a relative error of at most 0.001.
Values may be sent and summed in bfloat16 or wider, within the bound.
A program may use at most 64 MiB of HBM per device.

v0:
```python
import jax
import jax.numpy as jnp
from jax import lax
from jax.sharding import Mesh
from jax.sharding import PartitionSpec as P

SLOTS = 8
SHIFT_MOST = 2
ROW = ("row_0", "row_1", "row_2")
SLIDES_ROW = ("slides", "row_0", "row_1", "row_2")


def extended(array, sides, width):
    for axis, dim in sides:
        size, length = (lax.axis_size(axis), array.shape[dim])
        up = [(i, (i + 1) % size) for i in range(size - 1)]
        down = [(j, i) for i, j in up]
        last = lax.slice_in_dim(array, length - width, length, axis=dim)
        initial = lax.slice_in_dim(array, 0, width, axis=dim)
        before = lax.ppermute(last, axis, up)
        after = lax.ppermute(initial, axis, down)
        array = jnp.concatenate([before, array, after], axis=dim)
    return array


def in_order(pieces, dim):
    pieces = jnp.moveaxis(pieces, 0, dim)
    dims = pieces.shape
    return pieces.reshape(*dims[:dim], dims[dim] * dims[dim + 1], *dims[dim + 2 :])


def gather_in_order(array, axes, turns):
    pieces = array
    for k in turns:
        pieces = lax.all_gather(pieces, axes[k])
    done = turns[::-1]
    back = [done.index(k) for k in range(len(axes))]
    pieces = pieces.transpose(*back, *range(len(axes), pieces.ndim))
    return pieces.reshape(-1, *array.shape)


def whole_of(array, axes, turns, dim):
    return in_order(gather_in_order(array, axes, turns), dim)


def passed_along(array, axis, by):
    length = lax.axis_size(axis)
    pairs = [(i, i + by) for i in range(length) if 0 <= i + by < length]
    return lax.ppermute(array, axis, pairs)


def convolve(padded, conv_weight, conv_bias):
    tile_count = padded.shape[0]
    channels = conv_weight.shape[2]
    side = padded.shape[1] - 2
    pixels = padded.reshape(tile_count, side + 2, side + 2, channels)
    widened = jnp.concatenate(
        [pixels[:, :, 0:side], pixels[:, :, 1 : side + 1], pixels[:, :, 2 : side + 2]], axis=3
    )
    result = jnp.zeros((tile_count, side, side, channels), jnp.float32)
    for vertical in range(3):
        kernel = conv_weight[vertical].reshape(3 * channels, channels)
        result = result + jnp.einsum(
            "nhwk,ko->nhwo",
            widened[:, vertical : vertical + side],
            kernel,
            preferred_element_type=jnp.float32,
        )
    result = result + conv_bias.astype(jnp.float32)
    return result.astype(jnp.bfloat16).reshape(tile_count, side, side * channels)


def on_device(slide_pixels, tissue_mask, conv_weight, conv_bias):
    band_rows, grid_cols = tissue_mask.shape
    channels = conv_weight.shape[2]
    side = slide_pixels.shape[0] // band_rows
    tile_total = band_rows * grid_cols
    flat_mask = tissue_mask.reshape(tile_total)
    own_count = jnp.sum(flat_mask)
    blocks = slide_pixels.reshape(band_rows, side, grid_cols, side, channels)
    keeps = tissue_mask.astype(jnp.bfloat16)[:, None, :, None, None]
    masked = (blocks * keeps).reshape(band_rows * side, grid_cols * side * channels)
    haloed = extended(masked, ((ROW, 0),), 1)
    widened = haloed.reshape(band_rows * side + 2, grid_cols * side, channels)
    widened = jnp.pad(widened, ((0, 0), (1, 1), (0, 0)))
    pieces = []
    for tile_row in range(band_rows):
        for tile_col in range(grid_cols):
            window = widened[
                tile_row * side : tile_row * side + side + 2,
                tile_col * side : tile_col * side + side + 2,
            ]
            pieces.append(window.reshape(side + 2, (side + 2) * channels))
    padded_tiles = jnp.stack(pieces)
    device = lax.axis_index(ROW)
    table = whole_of(own_count.reshape(1), (("row_0", "row_1"), "row_2"), (0, 1), 0)
    lower = jnp.arange(table.shape[0], dtype=jnp.int32) < device
    earlier = jnp.sum(jnp.where(lower, table, jnp.zeros_like(table)))
    order = jnp.argsort(1 - flat_mask, stable=True)
    first_rank = device * SLOTS

    def select(start, amount):
        ranks = start + jnp.arange(amount, dtype=jnp.int32)
        local = ranks - earlier
        present = (local >= 0) & (local < own_count)
        where_tile = jnp.take(order, jnp.clip(local, 0, tile_total - 1), axis=0)
        chosen = jnp.take(padded_tiles, where_tile, axis=0)
        return (chosen, present)

    kept, kept_live = select(first_rank, SLOTS)
    onward, onward_live = select(first_rank + SLOTS, SHIFT_MOST)
    upper = SLOTS - SHIFT_MOST

    def keep_live(values, live):
        return jnp.where(live[:, None, None], values, jnp.zeros_like(values))

    from_prev = passed_along(keep_live(onward, onward_live), ROW, 1)
    owned = keep_live(kept, kept_live) + jnp.pad(from_prev, ((0, upper), (0, 0), (0, 0)))
    return convolve(owned, conv_weight, conv_bias)


def solution(mesh):
    finer = Mesh(
        mesh.devices.reshape(mesh.shape["slides"], 4, 16, 2), ("slides", "row_0", "row_1", "row_2")
    )
    return jax.shard_map(
        on_device,
        mesh=finer,
        in_specs=(P(SLIDES_ROW, None), P(SLIDES_ROW, None), P(), P()),
        out_specs=P(SLIDES_ROW, None, None),
        check_vma=False,
    )
```

profile of v0, /device:TPU:46, one launch (start us, length us, event | category | flops | bytes accessed | tf_op | source)
XLA Modules:
  0.0 154.7 jit_solution(15150391593055640642)
XLA Ops:
  0.0 1.4 fusion.19
  1.4 3.0 %mul.23 = bf16[2,32,8,32,64]{4,3,2,1,0:T(8,128)(2,1)} broadcast(bf16[2,8]{1,0:T(2,128)(2,1)S(1)} %get-tuple-element.34), dimensions={0,2} | broadcast | bytes 2097184 | tf_op jit(solution)/shard_map/mul | solution.py:82
  4.4 6.0 %mul.24 = bf16[64,16384]{1,0:T(8,128)(2,1)} reshape(bf16[2,32,8,32,64]{4,3,2,1,0:T(8,128)(2,1)} %mul.23) | data formatting | bytes 4194304 | tf_op jit(solution)/shard_map/mul | solution.py:82
  10.4 2.7 %mul.25 = bf16[64,16384]{1,0:T(8,128)(2,1)S(1)} multiply(bf16[64,16384]{1,0:T(8,128)(2,1)} %param.4, bf16[64,16384]{1,0:T(8,128)(2,1)} %mul.24) | non-fusion elementwise | flops 1048576 | bytes 6291456 | tf_op jit(solution)/shard_map/mul | solution.py:82
  13.2 2.0 %collective-permute-start = (bf16[1,16384]{1,0:T(2,128)(2,1)S(1)}, bf16[1,16384]{1,0:T(2,128)(2,1)S(1)}, u32[]{:S(2)}, u32[]{:S(2)}) collective-permute-start(bf16[1,16384]{1,0:T(2,128)(2,1)S(1)} %get-tuple-element.28), channel_id=1, source_target_pairs={{0,1},{1,2},{2,3},{3,4},{4,5},{5,6},{6,7},{7,8},{8,9},{9,10},{10,1... | collective-permute-start | bytes 98312 | tf_op jit(solution)/shard_map/ppermute | solution.py:20
  15.2 24.0 %collective-permute-start.1 = (bf16[1,16384]{1,0:T(2,128)(2,1)S(1)}, bf16[1,16384]{1,0:T(2,128)(2,1)S(1)}, u32[]{:S(2)}, u32[]{:S(2)}) collective-permute-start(bf16[1,16384]{1,0:T(2,128)(2,1)S(1)} %get-tuple-element.29), channel_id=1, source_target_pairs={{1,0},{2,1},{3,2},{4,3},{5,4},{6,5},{7,6},{8,7},{9,8},{10,9},{11,1... | collective-permute-start | bytes 98312 | tf_op jit(solution)/shard_map/ppermute | solution.py:21
  40.4 1.3 dynamic-update-slice
  41.7 23.2 %all-reduce.2 = s32[64]{0:T(128)S(1)} all-reduce(s32[64]{0:T(128)S(1)} %dynamic-update-slice), channel_id=1, replica_groups=mesh['slides'=2,'row_0'=4,'row_1'=16,'row_2'=2] {'row_0','row_1'}, use_global_device_ids=true, to_apply=%add.2 | all-reduce | flops 64 | bytes 512
  65.9 1.8 %all-reduce.3 = s32[128]{0:T(128)S(1)} all-reduce(s32[128]{0:T(128)S(1)} %dynamic-update-slice.1), channel_id=2, replica_groups=mesh['slides'=2,'row_0'=4,'row_1'=16,'row_2'=2] {'row_2'}, use_global_device_ids=true, to_apply=%add.3 | all-reduce | flops 128 | bytes 1024
  69.3 1.2 sort.17
  71.9 1.4 compare_and_fusion.2
  75.3 1.4 compare_and_fusion
  76.7 5.7 %concatenate.30 = bf16[64,256,64]{2,1,0:T(8,128)(2,1)} reshape(bf16[64,16384]{1,0:T(8,128)(2,1)S(1)} %mul.25) | data formatting | bytes 4194304 | tf_op jit(solution)/shard_map/concatenate | solution.py:22
  83.0 4.5 %constant_dynamic-update-slice_fusion.3 = (bf16[65,256,64]{2,1,0:T(8,128)(2,1)S(1)}, bf16[65,256,64]{2,1,0:T(8,128)(2,1)S(1)}) fusion(bf16[64,256,64]{2,1,0:T(8,128)(2,1)} %concatenate.30, bf16[65,256,64]{2,1,0:T(8,128)(2,1)S(1)} %constant_dynamic-update-slice_fusion.1), kind=kLoop, calls=%fused_computation.19 | loop fusion | bytes 10485760
  87.6 6.4 %fusion.5 = bf16[66,258,64]{2,1,0:T(8,128)(2,1)} fusion(bf16[1,256,64]{2,1,0:T(8,128)(2,1)S(1)} %concatenate.31, bf16[64,256,64]{2,1,0:T(8,128)(2,1)S(1)} %copy-done, bf16[1,256,64]{2,1,0:T(8,128)(2,1)S(1)} %concatenate.29), kind=kLoop, calls=%fused_computation.11 | loop fusion | flops 13077504 | bytes 4342272 | tf_op jit(solution)/shard_map/concatenate | solution.py:22
  94.1 1.0 fusion.14
  95.3 1.6 %fusion.13 = (bf16[34,34,64]{2,1,0:T(8,128)(2,1)S(1)}, bf16[34,34,64]{2,1,0:T(8,128)(2,1)S(1)}, bf16[34,34,64]{2,1,0:T(8,128)(2,1)S(1)}, bf16[34,34,64]{2,1,0:T(8,128)(2,1)S(1)}) fusion(bf16[66,258,64]{2,1,0:T(8,128)(2,1)} %fusion.5), kind=kLoop, calls=%fused_computation.67 | loop fusion | bytes 1183744 | tf_op jit(solution)/shard_map/slice | solution.py:89
  104.4 2.7 %fusion.15 = (bf16[34,34,64]{2,1,0:T(8,128)(2,1)S(1)}, bf16[34,34,64]{2,1,0:T(8,128)(2,1)S(1)}, bf16[34,34,64]{2,1,0:T(8,128)(2,1)S(1)}, bf16[34,34,64]{2,1,0:T(...) fusion(bf16[65,256,64]{2,1,0:T(8,128)(2,1)} %copy-done.2), kind=kLoop, calls=%fused_computation.69 | loop fusion | bytes 1775616 | tf_op jit(solution)/shard_map/slice | solution.py:89
  113.5 0.9 constant_dynamic-update-slice_fusion.18
  114.5 0.9 constant_dynamic-update-slice_fusion.17
  116.3 0.9 constant_dynamic-update-slice_fusion.15
  126.5 2.2 %collective-permute-start.2 = (bf16[2,34,2176]{2,1,0:T(8,128)(2,1)S(1)}, bf16[2,34,2176]{2,1,0:T(8,128)(2,1)}, u32[]{:S(2)}, u32[]{:S(2)}) collective-permute-start(bf16[2,34,2176]{2,1,0:T(8,128)(2,1)S(1)} %select_select_fusion), channel_id=1, source_target_pairs={{0,1},{1,2},{2,3},{3,4},{4,5},{5,6},{6,7},{7,8},{8,9},{9,10},{10,1... | collective-permute-start | bytes 887816 | tf_op jit(solution)/shard_map/ppermute | solution.py:49
  128.7 1.5 fusion.18
  130.2 2.5 %gather_fusion.1 = bf16[8,34,2176]{2,1,0:T(8,128)(2,1)S(1)} fusion(bf16[16,34,2176]{2,1,0:T(8,128)(2,1)} %copy-done.1, s32[1024]{0:T(1024)S(1)} %pad_clamp_fusion.2), kind=kCustom, calls=%fused_computation.1 | custom fusion | bytes 2367520 | tf_op jit(solution)/shard_map/jit(_take)/gather | solution.py:107
  132.8 4.6 %collective-permute-done.2 = bf16[2,34,2176]{2,1,0:T(8,128)(2,1)} collective-permute-done((bf16[2,34,2176]{2,1,0:T(8,128)(2,1)S(1)}, bf16[2,34,2176]{2,1,0:T(8,128)(2,1)}, u32[]{:S(2)}, u32[]{:S(2)}) %collective-permute-start.2) | collective-permute-done | bytes 295968 | tf_op jit(solution)/shard_map/ppermute | solution.py:49
  137.4 2.4 %pad_add_fusion = bf16[8,34,2176]{2,1,0:T(8,128)(2,1)} fusion(bf16[2,34,2176]{2,1,0:T(8,128)(2,1)} %collective-permute-done.2, bf16[8,34,2176]{2,1,0:T(8,128)(2,1)S(1)} %gather_fusion.1, pred[8]{0:T(512)(128)(4,1)S(1)} %get-tuple-element.38, pred[8]{0:T(512)(128)(4,1)S(1)} %get-tuple-element.39), kind=kLoop, calls=%fused_computation.14 | loop fusion | flops 1775616 | bytes 2663440 | tf_op jit(solution)/shard_map/add | solution.py:118
  139.8 3.3 %reshape.219 = bf16[8,34,34,64]{3,2,1,0:T(8,128)(2,1)S(1)} reshape(bf16[8,34,2176]{2,1,0:T(8,128)(2,1)} %pad_add_fusion) | data formatting | bytes 2367488 | tf_op jit(solution)/shard_map/reshape | solution.py:56
  143.1 1.6 %fusion.16 = (bf16[8,34,32,64]{3,2,1,0:T(8,128)(2,1)S(1)}, bf16[8,34,32,64]{3,2,1,0:T(8,128)(2,1)S(1)}, bf16[8,34,32,64]{3,2,1,0:T(8,128)(2,1)S(1)}) fusion(bf16[8,34,34,64]{3,2,1,0:T(8,128)(2,1)S(1)} %reshape.219), kind=kLoop, calls=%fused_computation.70 | loop fusion | bytes 6684672 | tf_op jit(solution)/shard_map/slice | solution.py:58
  144.7 2.4 %fusion.11 = f32[8,32,32,64]{3,2,1,0:T(8,128)S(1)} fusion(bf16[192,64,1,1]{1,0,3,2:T(8,128)(2,1)S(1)} %bitcast.39, bf16[8,34,32,64]{3,2,1,0:T(8,128)(2,1)S(1)} %get-tuple-element.27, bf16[8,34,32,64]{3,2,1,0:T(8,128)(2,1)S(1)} %get-tuple-element.26, bf16[8,34,32,64]{3,2,1,0:T(8,128)(2,1)S(1)} %get-tuple-element.25), kind=kOutput, calls=%fused_computation.65 | convolution fusion | flops 211353600 | bytes 5464064 | tf_op jit(solution)/shard_map/nhwk,ko->nhwo/dot_general | solution.py:63
  147.1 2.3 %fusion.12 = f32[8,32,32,64]{3,2,1,0:T(8,128)S(1)} fusion(bf16[192,64,1,1]{1,0,3,2:T(8,128)(2,1)S(1)} %bitcast.38, bf16[8,34,32,64]{3,2,1,0:T(8,128)(2,1)S(1)} %get-tuple-element.27, bf16[8,34,32,64]{3,2,1,0:T(8,128)(2,1)S(1)} %get-tuple-element.26, bf16[8,34,32,64]{3,2,1,0:T(8,128)(2,1)S(1)} %get-tuple-element.25), kind=kOutput, calls=%fused_computation.66 | convolution fusion | flops 211353600 | bytes 5464064 | tf_op jit(solution)/shard_map/nhwk,ko->nhwo/dot_general | solution.py:63
  149.5 2.8 %add_convert_fusion = bf16[8,32,32,64]{3,2,1,0:T(8,128)(2,1)S(1)} fusion(f32[8,32,32,64]{3,2,1,0:T(8,128)S(1)} %fusion.12, f32[8,32,32,64]{3,2,1,0:T(8,128)S(1)} %fusion.11, bf16[192,64,1,1]{1,0,3,2:T(8,128)(2,1)S(1)} %bitcast.37, f32[64]{0:T(128)S(1)} %convert_element_type.14, bf16[8,34,32,64]{3,2,1,0:T(8,128)(2,1)S(1)} %get-tuple-element.27, ...), kind=kOutput, calls=%fused_computation.13 | convolution fusion | flops 213450752 | bytes 8610048 | tf_op jit(solution)/shard_map/nhwk,ko->nhwo/dot_general | solution.py:63
  152.3 2.4 %reshape.169 = bf16[8,32,2048]{2,1,0:T(8,128)(2,1)} reshape(bf16[8,32,32,64]{3,2,1,0:T(8,128)(2,1)S(1)} %add_convert_fusion) | data formatting | bytes 2097152 | tf_op jit(solution)/shard_map/reshape | solution.py:70
  (76 shorter events, 31.5 us)
Async XLA Ops:
  10.4 28.8 %copy-start.7 = (u32[256]{0:T(256)S(1)}, u32[256]{0:T(256)}, u32[]{:S(2)}) copy-start(u32[256]{0:T(256)} %constant.98) | copy-start | bytes 3076
  10.4 29.5 %copy-start.6 = (u32[256]{0:T(256)S(1)}, u32[256]{0:T(256)}, u32[]{:S(2)}) copy-start(u32[256]{0:T(256)} %constant.93) | copy-start | bytes 3076
  13.2 69.2 %collective-permute-start = (bf16[1,16384]{1,0:T(2,128)(2,1)S(1)}, bf16[1,16384]{1,0:T(2,128)(2,1)S(1)}, u32[]{:S(2)}, u32[]{:S(2)}) collective-permute-start(bf16[1,16384]{1,0:T(2,128)(2,1)S(1)} %get-tuple-element.28), channel_id=1, source_target_pairs={{0,1},{1,2},{2,3},{3,4},{4,5},{5,6},{6,7},{7,8},{8,9},{9,10},{10,1... | collective-permute-start | bytes 98312 | tf_op jit(solution)/shard_map/ppermute | solution.py:20
  15.2 67.5 %collective-permute-start.1 = (bf16[1,16384]{1,0:T(2,128)(2,1)S(1)}, bf16[1,16384]{1,0:T(2,128)(2,1)S(1)}, u32[]{:S(2)}, u32[]{:S(2)}) collective-permute-start(bf16[1,16384]{1,0:T(2,128)(2,1)S(1)} %get-tuple-element.29), channel_id=1, source_target_pairs={{1,0},{2,1},{3,2},{4,3},{5,4},{6,5},{7,6},{8,7},{9,8},{10,9},{11,1... | collective-permute-start | bytes 98312 | tf_op jit(solution)/shard_map/ppermute | solution.py:21
  76.7 5.7 %copy-start.5 = (bf16[64]{0:T(256)(128)(2,1)S(1)}, bf16[64]{0:T(256)(128)(2,1)}, u32[]{:S(2)}) copy-start(bf16[64]{0:T(256)(128)(2,1)} %param.7) | copy-start | bytes 388
  83.0 4.5 %copy-start = (bf16[64,256,64]{2,1,0:T(8,128)(2,1)S(1)}, bf16[64,256,64]{2,1,0:T(8,128)(2,1)}, u32[]{:S(2)}) copy-start(bf16[64,256,64]{2,1,0:T(8,128)(2,1)} %concatenate.30) | copy-start | bytes 6291460
  87.6 6.5 %copy-start.2 = (bf16[65,256,64]{2,1,0:T(8,128)(2,1)}, bf16[65,256,64]{2,1,0:T(8,128)(2,1)S(1)}, u32[]{:S(2)}) copy-start(bf16[65,256,64]{2,1,0:T(8,128)(2,1)S(1)} %get-tuple-element.24) | copy-start | bytes 6389764
  125.8 2.9 %copy-start.1 = (bf16[16,34,2176]{2,1,0:T(8,128)(2,1)}, bf16[16,34,2176]{2,1,0:T(8,128)(2,1)S(1)}, u32[]{:S(2)}) copy-start(bf16[16,34,2176]{2,1,0:T(8,128)(2,1)S(1)} %constant_dynamic-update-slice_fusion.4) | copy-start | bytes 7102468
  126.5 10.9 %collective-permute-start.2 = (bf16[2,34,2176]{2,1,0:T(8,128)(2,1)S(1)}, bf16[2,34,2176]{2,1,0:T(8,128)(2,1)}, u32[]{:S(2)}, u32[]{:S(2)}) collective-permute-start(bf16[2,34,2176]{2,1,0:T(8,128)(2,1)S(1)} %select_select_fusion), channel_id=1, source_target_pairs={{0,1},{1,2},{2,3},{3,4},{4,5},{5,6},{6,7},{7,8},{8,9},{9,10},{10,1... | collective-permute-start | bytes 887816 | tf_op jit(solution)/shard_map/ppermute | solution.py:49
  143.1 1.6 %copy-start.4 = (bf16[1,3,64,64]{3,2,1,0:T(8,128)(2,1)S(1)}, bf16[1,3,64,64]{3,2,1,0:T(8,128)(2,1)}, u32[]{:S(2)}) copy-start(bf16[1,3,64,64]{3,2,1,0:T(8,128)(2,1)} %get-tuple-element.32) | copy-start | bytes 73732
  144.7 2.4 %copy-start.3 = (bf16[1,3,64,64]{3,2,1,0:T(8,128)(2,1)S(1)}, bf16[1,3,64,64]{3,2,1,0:T(8,128)(2,1)}, u32[]{:S(2)}) copy-start(bf16[1,3,64,64]{3,2,1,0:T(8,128)(2,1)} %get-tuple-element.31) | copy-start | bytes 73732
where the time goes:
time: 157 us; the launch traced here: 155 us
  local copies, waits for them, and re-layouts  67.5 us (43%)
  starting transfers between devices  28.1 us (18%)
  blocking collectives  25.1 us (16%)
  other arithmetic  20.9 us (13%)
  matrix products  7.52 us (5%)
  waiting for transfers between devices  4.62 us (3%)
    unnamed x2, blocking collectives  25.1 us
    ppermute x1, starting transfers between devices, extended(): after = lax.ppermute(initial, axis, down)  24 us
    unnamed x39, local copies, waits for them, and re-layouts  20.5 us
    another operation x17, local copies, waits for them, and re-layouts, on_device(): padded_tiles = jnp.stack(pieces)  13.3 us
    mul x2, local copies, waits for them, and re-layouts, on_device(): blocks * keeps  8.98 us
    dot_general x3, matrix products, convolve(): jnp.einsum('nhwk,ko->nhwo', widened[:, vertical:vertical + side], kernel,...  7.52 us
    concatenate x1, other arithmetic, extended(): array = jnp.concatenate([before, array, after], axis=dim)  6.45 us
    concatenate x4, local copies, waits for them, and re-layouts, extended(): array = jnp.concatenate([before, array, after], axis=dim)  5.9 us
  transfers between devices with their start and end apart: 3, of which 1 were waited for; matrix products, arithmetic and copies ran while one was open for 14% of the time, Pallas kernels for 0%

commit v1 on v0

v1 whole, which is shorter than its diff:
```python
import functools

import jax
import jax.numpy as jnp
from jax import lax
from jax.experimental import pallas as pl
from jax.experimental.pallas import tpu as pltpu
from jax.sharding import Mesh
from jax.sharding import PartitionSpec as P

SLOTS = 8
SHIFT_MOST = 2
ROW = ("row_0", "row_1", "row_2")
SLIDES_ROW = ("slides", "row_0", "row_1", "row_2")
MESH = pl.DeviceIdType.MESH
LANES = 128
F32 = jnp.float32
BF16 = jnp.bfloat16
I32 = jnp.int32


def kernel(
    pixels,
    mask_in,
    weight_in,
    bias_in,
    out,
    band,
    mask,
    weight,
    bias,
    big,
    fat,
    lhs,
    done,
    edge_first,
    edge_last,
    first_row,
    last_row,
    first_send,
    last_send,
    above_in,
    below_in,
    above,
    below,
    tile_send,
    tile_in,
    rim_work,
    rim_send,
    rim_in,
    note_send,
    note_in,
    counts,
    line_send,
    line_in,
    order,
    local_sem,
    send_sem,
    recv_sem,
    many_sem,
):
    x, z, c = (lax.axis_index(axis) for axis in ROW)
    planes, ring, cores = (lax.axis_size(axis) for axis in ROW)
    rows_dev, cols = mask_in.shape
    side = pixels.shape[0] // rows_dev
    tiles = rows_dev * cols
    chunks = pixels.shape[1] // (cols * LANES)
    groups = chunks // 2
    total = cols * chunks
    rank = (x * ring + z) * cores + c
    group_size = planes * ring * cores
    early = z == 0
    hub = (z == 0) & (c == 1)
    pair = x + 1 - 2 * (x % 2)

    def place(r):
        r = (r + group_size) % group_size
        return {"row_0": r // (ring * cores), "row_1": (r // cores) % ring, "row_2": r % cores}

    nxt, prv = place(rank + 1), place(rank - 1)

    def tell(where):
        pl.semaphore_signal(barrier, inc=1, device_id=where, device_id_type=MESH)

    barrier = pltpu.get_barrier_semaphore()
    copies = [
        pltpu.make_async_copy(mask_in, mask, local_sem.at[0]),
        pltpu.make_async_copy(pixels.at[48:64], band.at[48:64], local_sem.at[1]),
        pltpu.make_async_copy(pixels.at[0:16], band.at[0:16], local_sem.at[2]),
        pltpu.make_async_copy(pixels.at[16:48], band.at[16:48], local_sem.at[3]),
        pltpu.make_async_copy(weight_in, weight, local_sem.at[4]),
        pltpu.make_async_copy(bias_in, bias, local_sem.at[5]),
    ]
    for copy in copies:
        copy.start()
    tell(nxt)
    tell(prv)

    @pl.when(hub)
    def _():
        tell({"row_0": pair, "row_1": z, "row_2": c})
        tell({"row_0": x, "row_1": z, "row_2": 0})
        tell({"row_0": pair, "row_1": z, "row_2": 0})

        def spread(k, _):
            for core in range(2):
                tell({"row_0": x, "row_1": k, "row_2": core})
                tell({"row_0": pair, "row_1": k, "row_2": core})
            return 0

        lax.fori_loop(1, ring, spread, 0)

    copies[0].wait()
    held = [mask[t // cols, t % cols] for t in range(tiles)]
    upto = []
    running = jnp.int32(0)
    for t in range(tiles):
        running = running + held[t]
        upto.append(running)
    own_count = running

    def nth(k):
        return sum(((upto[t] <= k).astype(I32) for t in range(tiles - 1)), jnp.int32(0))

    local = (x % 2) * (ring * cores) + z * cores + c
    counts[pl.ds(local, 1), :] = jnp.broadcast_to(own_count, (1, LANES))
    sent_tiles = [nth(own_count - SHIFT_MOST + a) for a in range(SHIFT_MOST)]
    for a in range(SHIFT_MOST):
        note_send[a : a + 1, :] = jnp.broadcast_to(sent_tiles[a], (1, LANES))
    for k in range(SLOTS):
        order[k] = nth(jnp.int32(k))

    def keep(row, col):
        inside = (col >= 0) & (col < cols)
        return jnp.where(inside, mask[row, jnp.clip(col, 0, cols - 1)], 0).astype(F32)

    lane = lax.broadcasted_iota(I32, (1, LANES), 1)
    lower = lane < LANES // 2

    copies[1].wait()
    copies[2].wait()
    zeros8 = jnp.zeros((8, LANES), F32)
    for ref in (first_row, last_row, above, below):
        ref[0:8, :] = zeros8
        ref[8 + total : 16 + total, :] = zeros8
    for col in range(cols):
        top_keep = held[col].astype(F32)
        low_keep = held[(rows_dev - 1) * cols + col].astype(F32)
        for k in range(chunks):
            at = col * chunks + k
            span = slice(at * LANES, (at + 1) * LANES)
            top = band[0:16, span].astype(F32)[0:1, :] * top_keep
            low = band[48:64, span].astype(F32)[15:16, :] * low_keep
            first_row[8 + at : 9 + at, :] = top
            last_row[8 + at : 9 + at, :] = low
    first_send[...] = first_row[8 : 8 + total, :].astype(BF16)
    last_send[...] = last_row[8 : 8 + total, :].astype(BF16)
    copies[3].wait()

    def lanes_of(col, k):
        at = jnp.clip(col * chunks + k, 0, total - 1)
        return pl.ds(at * LANES, LANES)

    for a in range(SHIFT_MOST):
        row, col = sent_tiles[a] // cols, sent_tiles[a] % cols
        rows = pl.ds(row * side, side)
        for k in range(chunks):
            tile_send[a, k] = band[rows, lanes_of(col, k)]
        right = band[rows, lanes_of(col, chunks)].astype(F32) * keep(row, col + 1)
        left = band[rows, lanes_of(col, -1)].astype(F32) * keep(row, col - 1)
        tile_send[a, chunks] = jnp.where(lower, right, left).astype(BF16)

    def one(source, pick):
        return source.astype(F32)[pick : pick + 1, :]

    def inner_rim(row, pick, block, col):
        centre = keep(row, col)
        for k in range(chunks):
            yield one(band[block : block + 16, lanes_of(col, k)], pick) * centre
        right = one(band[block : block + 16, lanes_of(col, chunks)], pick) * keep(row, col + 1)
        left = one(band[block : block + 16, lanes_of(col, -1)], pick) * keep(row, col - 1)
        yield jnp.where(lower, right, left)

    def edge_rim(ref, col):
        step = col * (chunks // 8) + 1
        body = ref[pl.ds(step * 8, chunks), :]
        for k in range(chunks):
            yield body[k : k + 1, :]
        left = ref[pl.ds((step - 1) * 8, 8), :][7:8, :]
        right = ref[pl.ds((step + chunks // 8) * 8, 8), :][0:1, :]
        yield jnp.where(lower, right, left)

    def build_big():
        copies[4].wait()
        copies[5].wait()
        nothing = jnp.zeros((64, 64), BF16)
        for dy in range(3):
            taps = [weight[dy, dx] for dx in range(3)]
            for p in (0, 1, 2, 3, 4, -1):
                parts = [taps[p - q + 1] if 0 <= p - q + 1 < 3 else nothing for q in range(4)]
                at = dy * 384 + (p if p >= 0 else 5) * 64
                big[at : at + 64, :] = jnp.concatenate(parts, axis=1)

    def bias_row():
        short = bias[...].astype(F32).reshape(1, 64)
        return jnp.concatenate([short] * 4, axis=1)

    def multiply():
        for dy in range(3):
            rows = slice(7 + dy, 7 + dy + side)
            for g in range(groups):
                at = slice(g * side, (g + 1) * side)
                right = fat[2 * g + 2 if g < groups - 1 else chunks, rows, :]
                left = fat[2 * g - 1 if g > 0 else chunks, rows, :]
                lhs[at, dy * 384 : dy * 384 + 128] = fat[2 * g, rows, :].astype(BF16)
                lhs[at, dy * 384 + 128 : dy * 384 + 256] = fat[2 * g + 1, rows, :].astype(BF16)
                lhs[at, dy * 384 + 256 : dy * 384 + 384] = jnp.where(lower, right, left).astype(BF16)
        return jnp.dot(lhs[...], big[...], preferred_element_type=F32) + bias_row()

    def finish(result, slot):
        for g in range(groups):
            done[slot, :, g * 256 : (g + 1) * 256] = result[g * side : (g + 1) * side].astype(BF16)

    def own_tiles():
        build_big()
        for row in range(rows_dev):

            def tile(col, _, row=row):
                rows = slice(row * side, (row + 1) * side)
                for k in range(chunks):
                    fat[k, 8 : 8 + side, :] = band[rows, lanes_of(col, k)].astype(F32)
                right = band[rows, lanes_of(col, chunks)].astype(F32) * keep(row, col + 1)
                left = band[rows, lanes_of(col, -1)].astype(F32) * keep(row, col - 1)
                fat[chunks, 8 : 8 + side, :] = jnp.where(lower, right, left)
                if row == 0:
                    rim = inner_rim(1, 0, side, col)
                    for k, line in enumerate(rim):
                        fat[k, 7:8, :] = jnp.zeros((1, LANES), F32)
                        fat[k, 8 + side : 9 + side, :] = line
                else:
                    rim = inner_rim(0, 15, side - 16, col)
                    for k, line in enumerate(rim):
                        fat[k, 7:8, :] = line
                        fat[k, 8 + side : 9 + side, :] = jnp.zeros((1, LANES), F32)
                result = multiply()
                finish(result, row * cols + col)
                for g in range(groups):
                    if row == 0:
                        edge_first[col, g : g + 1, :] = result[g * side : g * side + 1]
                    else:
                        edge_last[col, g : g + 1, :] = result[(g + 1) * side - 1 : (g + 1) * side]
                return 0

            lax.fori_loop(0, cols, tile, 0)

    @pl.when(early)
    def _():
        own_tiles()

    @pl.when(jnp.logical_not(hub))
    def _():
        pl.semaphore_wait(barrier, 4)

    @pl.when(hub)
    def _():
        pl.semaphore_wait(barrier, 3)

    def remote(source, target, k, where):
        return pltpu.make_async_remote_copy(
            source, target, send_sem.at[k], recv_sem.at[k], device_id=where, device_id_type=MESH
        )

    mine = counts.at[pl.ds(local, 1)]

    def count_to(plane):
        return pltpu.make_async_remote_copy(
            mine, mine, many_sem.at[0], many_sem.at[1],
            device_id={"row_0": plane, "row_1": 0, "row_2": 1}, device_id_type=MESH,
        )

    count_to(pair).start()

    @pl.when(jnp.logical_not(hub))
    def _():
        count_to(x).start()

    note = remote(note_send, note_in, 0, nxt)
    down = remote(last_send, above_in, 1, nxt)
    up = remote(first_send, below_in, 2, prv)
    bodies = [remote(tile_send.at[a], tile_in.at[a], 3 + a, nxt) for a in range(SHIFT_MOST)]
    rims = remote(rim_send, rim_in, 5, nxt)
    note.start()
    down.start()
    for body in bodies:
        body.start()
    up.start()

    def send_rims():
        down.wait_recv()
        seen = jnp.where(rank > 0, 1, 0).astype(F32)
        above[8 : 8 + total, :] = above_in[...].astype(F32) * seen
        row, col = sent_tiles[0] // cols, sent_tiles[0] % cols
        high = row == 0
        for k, (outer, inner) in enumerate(zip(edge_rim(above, col), inner_rim(0, 15, side - 16, col))):
            rim_work[0, k : k + 1, :] = jnp.where(high, outer, inner)
        for k, line in enumerate(inner_rim(1, 0, side, col)):
            rim_work[1, k : k + 1, :] = line
        for k, line in enumerate(inner_rim(0, 15, side - 16, sent_tiles[1] % cols)):
            rim_work[2, k : k + 1, :] = line
        rim_send[...] = rim_work[...].astype(BF16)
        rims.start()

    send_rims()

    @pl.when(jnp.logical_not(early))
    def _():
        own_tiles()

    up.wait_recv()
    seen = jnp.where(rank < group_size - 1, 1, 0).astype(F32)
    below[8 : 8 + total, :] = below_in[...].astype(F32) * seen

    def join(ref, edge, dy, row, block, pick):
        half = total // 2
        even = ref[pl.ds(8, half, 2), :]
        odd = ref[pl.ds(9, half, 2), :]
        right = ref[pl.ds(10, half, 2), :]
        left = ref[pl.ds(7, half, 2), :]
        side_by = jnp.concatenate([even, odd, jnp.where(lower, right, left)], axis=1).astype(BF16)
        more = jnp.dot(side_by, big[dy * 384 : (dy + 1) * 384, :], preferred_element_type=F32)
        at_row = lax.broadcasted_iota(I32, (16, 256), 0) == pick
        for col in range(cols):
            whole = more[col * groups : (col + 1) * groups] + edge[col]
            for g in range(groups):
                span = slice(g * 256, (g + 1) * 256)
                old = done[row * cols + col, block : block + 16, span].astype(F32)
                new = jnp.where(at_row, whole[g : g + 1, :], old)
                done[row * cols + col, block : block + 16, span] = new.astype(BF16)

    join(above, edge_first, 0, 0, 0, 0)
    join(below, edge_last, 2, rows_dev - 1, side - 16, 15)

    @pl.when(hub)
    def _():
        others = counts.at[pl.ds(0, 2 * ring * cores - 1)]
        pltpu.make_async_copy(others, others, many_sem.at[1]).wait()
        table = counts[...]
        spot = lax.broadcasted_iota(I32, table.shape, 0) == lax.broadcasted_iota(I32, table.shape, 1)
        line_send[...] = jnp.sum(jnp.where(spot, table, 0), axis=0, keepdims=True)

        def line_to(k, core):
            return pltpu.make_async_remote_copy(
                line_send, line_in, many_sem.at[2], many_sem.at[3],
                device_id={"row_0": x, "row_1": k, "row_2": core}, device_id_type=MESH,
            )

        line_to(0, 0).start()

        def spread(k, _):
            for core in range(2):
                line_to(k, core).start()
            return 0

        lax.fori_loop(1, ring, spread, 0)

    note.wait_recv()
    rims.wait_recv()
    for a in range(SHIFT_MOST):
        came = jnp.max(note_in[a : a + 1, :])
        row, col = came // cols, came % cols
        bodies[a].wait_recv()
        for k in range(chunks + 1):
            fat[k, 8 : 8 + side, :] = tile_in[a, k].astype(F32)
        over = rim_in[2 * a].astype(F32)
        under = rim_in[1].astype(F32)
        for k, line in enumerate(edge_rim(first_row, col)):
            fat[k, 7:8, :] = over[k : k + 1, :]
            if a == 0:
                line = jnp.where(row == rows_dev - 1, line, under[k : k + 1, :])
            fat[k, 8 + side : 9 + side, :] = line
        finish(multiply(), tiles + a)

    @pl.when(jnp.logical_not(hub))
    def _():
        pltpu.make_async_copy(line_in, line_in, many_sem.at[3]).wait()

    line = jnp.where(hub, line_send[...], line_in[...])
    before = jnp.sum(jnp.where(lane < local, line, 0))
    whole = jnp.sum(line)
    start = jnp.where(x < planes // 2, 0, SLOTS * ring * cores * 2 - whole)
    excess = start + before - SLOTS * local
    excess = jnp.clip(excess, 0, SHIFT_MOST)
    for j in range(SLOTS):
        own = order[jnp.clip(j - excess, 0, SLOTS - 1)]
        came = tiles + SHIFT_MOST - excess + j
        out[j] = done[jnp.clip(jnp.where(j < excess, came, own), 0, tiles + SHIFT_MOST - 1)]

    for copy in (note, down, up, *bodies, rims):
        copy.wait_send()
    count_to(pair).wait_send()

    @pl.when(jnp.logical_not(hub))
    def _():
        count_to(x).wait_send()

    @pl.when(hub)
    def _():
        sent = counts.at[pl.ds(0, ring * cores - 1)]
        pltpu.make_async_copy(sent, sent, many_sem.at[2]).wait()


def on_device(slide_pixels, tissue_mask, conv_weight, conv_bias):
    rows_dev, cols = tissue_mask.shape
    side = slide_pixels.shape[0] // rows_dev
    width = slide_pixels.shape[1] // cols
    chunks = width // LANES
    groups = chunks // 2
    total = cols * chunks
    tiles = rows_dev * cols
    pair_size = 2 * lax.axis_size("row_1") * lax.axis_size("row_2")
    strip = pltpu.VMEM((total + 16, LANES), F32)
    packed = pltpu.VMEM((total, LANES), BF16)
    rim = pltpu.VMEM((3, 32, LANES), BF16)
    tile_pair = pltpu.VMEM((SHIFT_MOST, chunks + 1, side, LANES), BF16)
    edge = pltpu.VMEM((cols, groups, 256), F32)
    return pl.pallas_call(
        kernel,
        out_shape=pltpu.VMEM((SLOTS, side, width), BF16),
        in_specs=[pl.BlockSpec(memory_space=pltpu.HBM)] * 4,
        out_specs=pl.BlockSpec(memory_space=pltpu.VMEM),
        scratch_shapes=[
            pltpu.VMEM(slide_pixels.shape, BF16),
            pltpu.SMEM((rows_dev, cols), I32),
            pltpu.VMEM(conv_weight.shape, BF16),
            pltpu.VMEM(conv_bias.shape, BF16),
            pltpu.VMEM((3 * 384, 256), BF16),
            pltpu.VMEM((chunks + 1, 48, LANES), F32),
            pltpu.VMEM((groups * side, 3 * 384), BF16),
            pltpu.VMEM((tiles + SHIFT_MOST, side, width), BF16),
            edge,
            edge,
            strip,
            strip,
            packed,
            packed,
            packed,
            packed,
            strip,
            strip,
            tile_pair,
            tile_pair,
            pltpu.VMEM((3, 32, LANES), F32),
            rim,
            rim,
            pltpu.VMEM((SHIFT_MOST, LANES), I32),
            pltpu.VMEM((SHIFT_MOST, LANES), I32),
            pltpu.VMEM((pair_size, LANES), I32),
            pltpu.VMEM((1, LANES), I32),
            pltpu.VMEM((1, LANES), I32),
            pltpu.SMEM((SLOTS,), I32),
            pltpu.SemaphoreType.DMA((6,)),
            pltpu.SemaphoreType.DMA((6,)),
            pltpu.SemaphoreType.DMA((6,)),
            pltpu.SemaphoreType.DMA((4,)),
        ],
        compiler_params=pltpu.CompilerParams(
            collective_id=0, has_side_effects=True, vmem_limit_bytes=24 * 1024 * 1024
        ),
        name="tissue_tiles",
    )(slide_pixels, tissue_mask, conv_weight, conv_bias)


def solution(mesh):
    finer = Mesh(
        mesh.devices.reshape(mesh.shape["slides"], 4, 16, 2), ("slides", "row_0", "row_1", "row_2")
    )
    return jax.shard_map(
        on_device,
        mesh=finer,
        in_specs=(P(SLIDES_ROW, None), P(SLIDES_ROW, None), P(), P()),
        out_specs=P(SLIDES_ROW, None, None),
        check_vma=False,
    )
```

time: 157 us -> 37.1 us (0.24)
  the two profiles are of different devices: /device:TPU:46 before, /device:TPU:40 now
where the time goes in v1:
time: 37.1 us; the launch traced here: 36.9 us
  Pallas kernels  32.1 us (87%)
  local copies, waits for them, and re-layouts  4.81 us (13%)
    pallas_call x1, Pallas kernels, on_device(): pl.pallas_call(kernel, out_shape=pltpu.VMEM((SLOTS, side, width), BF16),...  32.1 us
    unnamed x9, local copies, waits for them, and re-layouts  4.81 us

profile of v1, /device:TPU:40, one launch (start us, length us, event | category | flops | bytes accessed | tf_op | source)
XLA Modules:
  0.0 36.9 jit_solution(1109485108465569253)
XLA Ops:
  0.0 0.0 copy-start
  0.0 1.6 %copy-done = bf16[64,16384]{1,0:T(8,128)(2,1)S(1)} copy-done((bf16[64,16384]{1,0:T(8,128)(2,1)S(1)}, bf16[64,16384]{1,0:T(8,128)(2,1)}, u32[]{:S(2)}) %copy-start) | copy-done | bytes 2097176
  1.6 0.0 copy-start.1
  1.6 0.9 %copy-done.1 = bf16[3,3,64,64]{3,2,1,0:T(8,128)(2,1)S(1)} copy-done((bf16[3,3,64,64]{3,2,1,0:T(8,128)(2,1)S(1)}, bf16[3,3,64,64]{3,2,1,0:T(8,128)(2,1)}, u32[]{:S(2)}) %copy-start.1) | copy-done | bytes 73752
  2.5 0.0 copy-start.2
  2.5 0.7 %copy-done.2 = s32[2,8]{1,0:T(2,128)S(1)} copy-done((s32[2,8]{1,0:T(2,128)S(1)}, s32[2,8]{1,0:T(2,128)}, u32[]{:S(2)}) %copy-start.2) | copy-done | bytes 88
  3.2 0.0 copy-start.3
  3.2 0.7 %copy-done.3 = bf16[64]{0:T(256)(128)(2,1)S(1)} copy-done((bf16[64]{0:T(256)(128)(2,1)S(1)}, bf16[64]{0:T(256)(128)(2,1)}, u32[]{:S(2)}) %copy-start.3) | copy-done | bytes 152
  3.8 32.1 %tissue_tiles.1 = bf16[8,32,2048]{2,1,0:T(8,128)(2,1)S(1)} custom-call(bf16[64,16384]{1,0:T(8,128)(2,1)S(1)} %copy-done, s32[2,8]{1,0:T(2,128)S(1)} %copy-done.2, bf16[3,3,64,64]{3,2,1,0:T(8,128)(2,1)S(1)} %copy-done.1, bf16[64]{0:T(256)(128)(2,1)S(1)} %copy-done.3), custom_call_target="tpu_custom_call" | custom-call | tf_op jit(solution)/shard_map/tissue_tiles/pallas_call | solution.py:426
  36.0 1.0 %copy.6 = bf16[8,32,2048]{2,1,0:T(8,128)(2,1)} copy(bf16[8,32,2048]{2,1,0:T(8,128)(2,1)S(1)} %tissue_tiles.1) | data formatting | bytes 2097152
Async XLA Ops:
  0.0 1.6 %copy-start = (bf16[64,16384]{1,0:T(8,128)(2,1)S(1)}, bf16[64,16384]{1,0:T(8,128)(2,1)}, u32[]{:S(2)}) copy-start(bf16[64,16384]{1,0:T(8,128)(2,1)} %pixels.1) | copy-start | bytes 6291460
  1.6 0.9 %copy-start.1 = (bf16[3,3,64,64]{3,2,1,0:T(8,128)(2,1)S(1)}, bf16[3,3,64,64]{3,2,1,0:T(8,128)(2,1)}, u32[]{:S(2)}) copy-start(bf16[3,3,64,64]{3,2,1,0:T(8,128)(2,1)} %weight_in.1) | copy-start | bytes 221188
  2.5 0.7 %copy-start.2 = (s32[2,8]{1,0:T(2,128)S(1)}, s32[2,8]{1,0:T(2,128)}, u32[]{:S(2)}) copy-start(s32[2,8]{1,0:T(2,128)} %mask_in.1) | copy-start | bytes 196
  3.2 0.7 %copy-start.3 = (bf16[64]{0:T(256)(128)(2,1)S(1)}, bf16[64]{0:T(256)(128)(2,1)}, u32[]{:S(2)}) copy-start(bf16[64]{0:T(256)(128)(2,1)} %bias_in.1) | copy-start | bytes 388

commit v2 on v1

--- a/solution.py
+++ b/solution.py
@@ -25,7 +25,8 @@
     weight_in,
     bias_in,
     out,
-    band,
+    top_band,
+    low_band,
     mask,
     weight,
     bias,
@@ -69,7 +70,8 @@
     total = cols * chunks
     rank = (x * ring + z) * cores + c
     group_size = planes * ring * cores
-    early = z == 0
+    follows, leads = rank > 0, rank < group_size - 1
+    early = (z == 0) & follows
     hub = (z == 0) & (c == 1)
     pair = x + 1 - 2 * (x % 2)
 
@@ -83,18 +85,24 @@
         pl.semaphore_signal(barrier, inc=1, device_id=where, device_id_type=MESH)
 
     barrier = pltpu.get_barrier_semaphore()
+    bands = (top_band, low_band)
     copies = [
         pltpu.make_async_copy(mask_in, mask, local_sem.at[0]),
-        pltpu.make_async_copy(pixels.at[48:64], band.at[48:64], local_sem.at[1]),
-        pltpu.make_async_copy(pixels.at[0:16], band.at[0:16], local_sem.at[2]),
-        pltpu.make_async_copy(pixels.at[16:48], band.at[16:48], local_sem.at[3]),
-        pltpu.make_async_copy(weight_in, weight, local_sem.at[4]),
-        pltpu.make_async_copy(bias_in, bias, local_sem.at[5]),
+        pltpu.make_async_copy(pixels.at[side : 2 * side], low_band, local_sem.at[1]),
+        pltpu.make_async_copy(pixels.at[0:side], top_band, local_sem.at[2]),
+        pltpu.make_async_copy(weight_in, weight, local_sem.at[3]),
+        pltpu.make_async_copy(bias_in, bias, local_sem.at[4]),
     ]
     for copy in copies:
         copy.start()
-    tell(nxt)
-    tell(prv)
+
+    @pl.when(leads)
+    def _():
+        tell(nxt)
+
+    @pl.when(follows)
+    def _():
+        tell(prv)
 
     @pl.when(hub)
     def _():
@@ -127,9 +135,6 @@
     sent_tiles = [nth(own_count - SHIFT_MOST + a) for a in range(SHIFT_MOST)]
     for a in range(SHIFT_MOST):
         note_send[a : a + 1, :] = jnp.broadcast_to(sent_tiles[a], (1, LANES))
-    for k in range(SLOTS):
-        order[k] = nth(jnp.int32(k))
-
     def keep(row, col):
         inside = (col >= 0) & (col < cols)
         return jnp.where(inside, mask[row, jnp.clip(col, 0, cols - 1)], 0).astype(F32)
@@ -137,37 +142,31 @@
     lane = lax.broadcasted_iota(I32, (1, LANES), 1)
     lower = lane < LANES // 2
 
-    copies[1].wait()
-    copies[2].wait()
-    zeros8 = jnp.zeros((8, LANES), F32)
-    for ref in (first_row, last_row, above, below):
-        ref[0:8, :] = zeros8
-        ref[8 + total : 16 + total, :] = zeros8
-    for col in range(cols):
-        top_keep = held[col].astype(F32)
-        low_keep = held[(rows_dev - 1) * cols + col].astype(F32)
-        for k in range(chunks):
-            at = col * chunks + k
-            span = slice(at * LANES, (at + 1) * LANES)
-            top = band[0:16, span].astype(F32)[0:1, :] * top_keep
-            low = band[48:64, span].astype(F32)[15:16, :] * low_keep
-            first_row[8 + at : 9 + at, :] = top
-            last_row[8 + at : 9 + at, :] = low
-    first_send[...] = first_row[8 : 8 + total, :].astype(BF16)
-    last_send[...] = last_row[8 : 8 + total, :].astype(BF16)
-    copies[3].wait()
-
     def lanes_of(col, k):
         at = jnp.clip(col * chunks + k, 0, total - 1)
         return pl.ds(at * LANES, LANES)
 
-    for a in range(SHIFT_MOST):
+    def outer_row(ref, send, row, block, pick):
+        for col in range(cols):
+            centre = held[row * cols + col].astype(F32)
+            for k in range(chunks):
+                at = col * chunks + k
+                line = bands[row][block : block + 16, at * LANES : (at + 1) * LANES].astype(F32)
+                ref[8 + at : 9 + at, :] = line[pick : pick + 1, :] * centre
+        send[...] = ref[8 : 8 + total, :].astype(BF16)
+
+    def stage(a):
         row, col = sent_tiles[a] // cols, sent_tiles[a] % cols
-        rows = pl.ds(row * side, side)
+        row = row if a == 0 else rows_dev - 1
+
+        def pixels_of(k):
+            low = low_band[:, lanes_of(col, k)]
+            return low if a else jnp.where(row == 0, top_band[:, lanes_of(col, k)], low)
+
         for k in range(chunks):
-            tile_send[a, k] = band[rows, lanes_of(col, k)]
-        right = band[rows, lanes_of(col, chunks)].astype(F32) * keep(row, col + 1)
-        left = band[rows, lanes_of(col, -1)].astype(F32) * keep(row, col - 1)
+            tile_send[a, k] = pixels_of(k)
+        right = pixels_of(chunks).astype(F32) * keep(row, col + 1)
+        left = pixels_of(-1).astype(F32) * keep(row, col - 1)
         tile_send[a, chunks] = jnp.where(lower, right, left).astype(BF16)
 
     def one(source, pick):
@@ -176,9 +175,9 @@
     def inner_rim(row, pick, block, col):
         centre = keep(row, col)
         for k in range(chunks):
-            yield one(band[block : block + 16, lanes_of(col, k)], pick) * centre
-        right = one(band[block : block + 16, lanes_of(col, chunks)], pick) * keep(row, col + 1)
-        left = one(band[block : block + 16, lanes_of(col, -1)], pick) * keep(row, col - 1)
+            yield one(bands[row][block : block + 16, lanes_of(col, k)], pick) * centre
+        right = one(bands[row][block : block + 16, lanes_of(col, chunks)], pick) * keep(row, col + 1)
+        left = one(bands[row][block : block + 16, lanes_of(col, -1)], pick) * keep(row, col - 1)
         yield jnp.where(lower, right, left)
 
     def edge_rim(ref, col):
@@ -191,8 +190,8 @@
         yield jnp.where(lower, right, left)
 
     def build_big():
+        copies[3].wait()
         copies[4].wait()
-        copies[5].wait()
         nothing = jnp.zeros((64, 64), BF16)
         for dy in range(3):
             taps = [weight[dy, dx] for dx in range(3)]
@@ -226,14 +225,14 @@
         for row in range(rows_dev):
 
             def tile(col, _, row=row):
-                rows = slice(row * side, (row + 1) * side)
+                band = bands[row]
                 for k in range(chunks):
-                    fat[k, 8 : 8 + side, :] = band[rows, lanes_of(col, k)].astype(F32)
-                right = band[rows, lanes_of(col, chunks)].astype(F32) * keep(row, col + 1)
-                left = band[rows, lanes_of(col, -1)].astype(F32) * keep(row, col - 1)
+                    fat[k, 8 : 8 + side, :] = band[:, lanes_of(col, k)].astype(F32)
+                right = band[:, lanes_of(col, chunks)].astype(F32) * keep(row, col + 1)
+                left = band[:, lanes_of(col, -1)].astype(F32) * keep(row, col - 1)
                 fat[chunks, 8 : 8 + side, :] = jnp.where(lower, right, left)
                 if row == 0:
-                    rim = inner_rim(1, 0, side, col)
+                    rim = inner_rim(1, 0, 0, col)
                     for k, line in enumerate(rim):
                         fat[k, 7:8, :] = jnp.zeros((1, LANES), F32)
                         fat[k, 8 + side : 9 + side, :] = line
@@ -253,18 +252,6 @@
 
             lax.fori_loop(0, cols, tile, 0)
 
-    @pl.when(early)
-    def _():
-        own_tiles()
-
-    @pl.when(jnp.logical_not(hub))
-    def _():
-        pl.semaphore_wait(barrier, 4)
-
-    @pl.when(hub)
-    def _():
-        pl.semaphore_wait(barrier, 3)
-
     def remote(source, target, k, where):
         return pltpu.make_async_remote_copy(
             source, target, send_sem.at[k], recv_sem.at[k], device_id=where, device_id_type=MESH
@@ -278,47 +265,108 @@
             device_id={"row_0": plane, "row_1": 0, "row_2": 1}, device_id_type=MESH,
         )
 
-    count_to(pair).start()
-
-    @pl.when(jnp.logical_not(hub))
-    def _():
-        count_to(x).start()
+    def arrive():
+        pl.semaphore_wait(barrier, 2 - hub.astype(I32) + follows.astype(I32) + leads.astype(I32))
+        count_to(pair).start()
+
+        @pl.when(jnp.logical_not(hub))
+        def _():
+            count_to(x).start()
 
     note = remote(note_send, note_in, 0, nxt)
     down = remote(last_send, above_in, 1, nxt)
     up = remote(first_send, below_in, 2, prv)
     bodies = [remote(tile_send.at[a], tile_in.at[a], 3 + a, nxt) for a in range(SHIFT_MOST)]
-    rims = remote(rim_send, rim_in, 5, nxt)
-    note.start()
-    down.start()
-    for body in bodies:
-        body.start()
-    up.start()
-
-    def send_rims():
-        down.wait_recv()
-        seen = jnp.where(rank > 0, 1, 0).astype(F32)
-        above[8 : 8 + total, :] = above_in[...].astype(F32) * seen
+    fixed_rims = remote(rim_send.at[0:2], rim_in.at[0:2], 5, nxt)
+    last_rim = remote(rim_send.at[2], rim_in.at[2], 6, nxt)
+    def send_low():
+        @pl.when(leads)
+        def _():
+            note.start()
+            bodies[1].start()
+            down.start()
+
+    def send_top():
+        stage(0)
+        inner_rims()
+
+        @pl.when(leads)
+        def _():
+            fixed_rims.start()
+            bodies[0].start()
+
+        outer_row(first_row, first_send, 0, 0, 0)
+
+        @pl.when(follows)
+        def _():
+            up.start()
+
+    def inner_rims():
+        for k, line in enumerate(inner_rim(1, 0, 0, sent_tiles[0] % cols)):
+            rim_work[0, k : k + 1, :] = line
+        for k, line in enumerate(inner_rim(0, 15, side - 16, sent_tiles[1] % cols)):
+            rim_work[1, k : k + 1, :] = line
+        rim_send[0:2] = rim_work[0:2].astype(BF16)
+
+    def send_last_rim():
+        @pl.when(follows)
+        def _():
+            down.wait_recv()
+            above[8 : 8 + total, :] = above_in[...].astype(F32)
+
+        @pl.when(jnp.logical_not(follows))
+        def _():
+            above[8 : 8 + total, :] = jnp.zeros((total, LANES), F32)
+
         row, col = sent_tiles[0] // cols, sent_tiles[0] % cols
-        high = row == 0
         for k, (outer, inner) in enumerate(zip(edge_rim(above, col), inner_rim(0, 15, side - 16, col))):
-            rim_work[0, k : k + 1, :] = jnp.where(high, outer, inner)
-        for k, line in enumerate(inner_rim(1, 0, side, col)):
-            rim_work[1, k : k + 1, :] = line
-        for k, line in enumerate(inner_rim(0, 15, side - 16, sent_tiles[1] % cols)):
-            rim_work[2, k : k + 1, :] = line
-        rim_send[...] = rim_work[...].astype(BF16)
-        rims.start()
-
-    send_rims()
+            rim_work[2, k : k + 1, :] = jnp.where(row == 0, outer, inner)
+        rim_send[2] = rim_work[2].astype(BF16)
+
+        @pl.when(leads)
+        def _():
+            last_rim.start()
+
+    zeros8 = jnp.zeros((8, LANES), F32)
+    for ref in (first_row, last_row, above, below):
+        ref[0:8, :] = zeros8
+        ref[8 + total : 16 + total, :] = zeros8
 
     @pl.when(jnp.logical_not(early))
     def _():
+        arrive()
+
+    copies[1].wait()
+    stage(1)
+    outer_row(last_row, last_send, rows_dev - 1, side - 16, 15)
+
+    @pl.when(early)
+    def _():
+        copies[2].wait()
         own_tiles()
-
-    up.wait_recv()
-    seen = jnp.where(rank < group_size - 1, 1, 0).astype(F32)
-    below[8 : 8 + total, :] = below_in[...].astype(F32) * seen
+        arrive()
+        send_low()
+        send_top()
+
+    @pl.when(jnp.logical_not(early))
+    def _():
+        send_low()
+        copies[2].wait()
+        send_top()
+        send_last_rim()
+        own_tiles()
+
+    for k in range(SLOTS):
+        order[k] = nth(jnp.int32(k))
+
+    @pl.when(leads)
+    def _():
+        up.wait_recv()
+        below[8 : 8 + total, :] = below_in[...].astype(F32)
+
+    @pl.when(jnp.logical_not(leads))
+    def _():
+        below[8 : 8 + total, :] = jnp.zeros((total, LANES), F32)
 
     def join(ref, edge, dy, row, block, pick):
         half = total // 2
@@ -337,8 +385,13 @@
                 new = jnp.where(at_row, whole[g : g + 1, :], old)
                 done[row * cols + col, block : block + 16, span] = new.astype(BF16)
 
+    join(below, edge_last, 2, rows_dev - 1, side - 16, 15)
+
+    @pl.when(early)
+    def _():
+        send_last_rim()
+
     join(above, edge_first, 0, 0, 0, 0)
-    join(below, edge_last, 2, rows_dev - 1, side - 16, 15)
 
     @pl.when(hub)
     def _():
@@ -363,22 +416,28 @@
 
         lax.fori_loop(1, ring, spread, 0)
 
-    note.wait_recv()
-    rims.wait_recv()
-    for a in range(SHIFT_MOST):
+    def taken(a):
         came = jnp.max(note_in[a : a + 1, :])
         row, col = came // cols, came % cols
         bodies[a].wait_recv()
         for k in range(chunks + 1):
             fat[k, 8 : 8 + side, :] = tile_in[a, k].astype(F32)
-        over = rim_in[2 * a].astype(F32)
-        under = rim_in[1].astype(F32)
+        over = rim_in[1 if a else 2].astype(F32)
+        under = rim_in[0].astype(F32)
         for k, line in enumerate(edge_rim(first_row, col)):
             fat[k, 7:8, :] = over[k : k + 1, :]
             if a == 0:
                 line = jnp.where(row == rows_dev - 1, line, under[k : k + 1, :])
             fat[k, 8 + side : 9 + side, :] = line
         finish(multiply(), tiles + a)
+
+    @pl.when(follows)
+    def _():
+        note.wait_recv()
+        fixed_rims.wait_recv()
+        taken(1)
+        last_rim.wait_recv()
+        taken(0)
 
     @pl.when(jnp.logical_not(hub))
     def _():
@@ -395,8 +454,15 @@
         came = tiles + SHIFT_MOST - excess + j
         out[j] = done[jnp.clip(jnp.where(j < excess, came, own), 0, tiles + SHIFT_MOST - 1)]
 
-    for copy in (note, down, up, *bodies, rims):
-        copy.wait_send()
+    @pl.when(leads)
+    def _():
+        for copy in (note, down, *bodies, fixed_rims, last_rim):
+            copy.wait_send()
+
+    @pl.when(follows)
+    def _():
+        up.wait_send()
+
     count_to(pair).wait_send()
 
     @pl.when(jnp.logical_not(hub))
@@ -407,6 +473,10 @@
     def _():
         sent = counts.at[pl.ds(0, ring * cores - 1)]
         pltpu.make_async_copy(sent, sent, many_sem.at[2]).wait()
+
+
+def in_hbm(array):
+    return pltpu.with_memory_space_constraint(array, pltpu.HBM)
 
 
 def on_device(slide_pixels, tissue_mask, conv_weight, conv_bias):
@@ -418,6 +488,7 @@
     total = cols * chunks
     tiles = rows_dev * cols
     pair_size = 2 * lax.axis_size("row_1") * lax.axis_size("row_2")
+    half = pltpu.VMEM((side, slide_pixels.shape[1]), BF16)
     strip = pltpu.VMEM((total + 16, LANES), F32)
     packed = pltpu.VMEM((total, LANES), BF16)
     rim = pltpu.VMEM((3, 32, LANES), BF16)
@@ -429,7 +500,8 @@
         in_specs=[pl.BlockSpec(memory_space=pltpu.HBM)] * 4,
         out_specs=pl.BlockSpec(memory_space=pltpu.VMEM),
         scratch_shapes=[
-            pltpu.VMEM(slide_pixels.shape, BF16),
+            half,
+            half,
             pltpu.SMEM((rows_dev, cols), I32),
             pltpu.VMEM(conv_weight.shape, BF16),
             pltpu.VMEM(conv_bias.shape, BF16),
@@ -458,16 +530,16 @@
             pltpu.VMEM((1, LANES), I32),
             pltpu.VMEM((1, LANES), I32),
             pltpu.SMEM((SLOTS,), I32),
-            pltpu.SemaphoreType.DMA((6,)),
-            pltpu.SemaphoreType.DMA((6,)),
-            pltpu.SemaphoreType.DMA((6,)),
+            pltpu.SemaphoreType.DMA((5,)),
+            pltpu.SemaphoreType.DMA((7,)),
+            pltpu.SemaphoreType.DMA((7,)),
             pltpu.SemaphoreType.DMA((4,)),
         ],
         compiler_params=pltpu.CompilerParams(
             collective_id=0, has_side_effects=True, vmem_limit_bytes=24 * 1024 * 1024
         ),
         name="tissue_tiles",
-    )(slide_pixels, tissue_mask, conv_weight, conv_bias)
+    )(*(in_hbm(array) for array in (slide_pixels, tissue_mask, conv_weight, conv_bias)))
 
 
 def solution(mesh):

time: 37.1 us -> 31.5 us (0.85)
  the two profiles are of different devices: /device:TPU:40 before, /device:TPU:160 now
where the time goes in v2:
time: 31.5 us; the launch traced here: 31.4 us
  Pallas kernels  30.4 us (97%)
  local copies, waits for them, and re-layouts  0.97 us (3%)
    pallas_call x1, Pallas kernels, on_device(): pl.pallas_call(kernel, out_shape=pltpu.VMEM((SLOTS, side, width), BF16),...  30.4 us
    unnamed x1, local copies, waits for them, and re-layouts  0.97 us

profile of v2, /device:TPU:160, one launch (start us, length us, event | category | flops | bytes accessed | tf_op | source)
XLA Modules:
  0.0 31.4 jit_solution(6650281389005444685)
XLA Ops:
  0.0 30.4 %tissue_tiles.1 = bf16[8,32,2048]{2,1,0:T(8,128)(2,1)S(1)} custom-call(bf16[64,16384]{1,0:T(8,128)(2,1)} %pixels.1, s32[2,8]{1,0:T(2,128)} %mask_in.1, bf16[3,3,64,64]{3,2,1,0:T(8,128)(2,1)} %weight_in.1, bf16[64]{0:T(256)(128)(2,1)} %bias_in.1), custom_call_target="tpu_custom_call" | custom-call | tf_op jit(solution)/shard_map/tissue_tiles/pallas_call | solution.py:497
  30.4 1.0 %copy.6 = bf16[8,32,2048]{2,1,0:T(8,128)(2,1)} copy(bf16[8,32,2048]{2,1,0:T(8,128)(2,1)S(1)} %tissue_tiles.1) | data formatting | bytes 2097152

commit v3 on v2

--- a/solution.py
+++ b/solution.py
@@ -71,7 +71,8 @@
     rank = (x * ring + z) * cores + c
     group_size = planes * ring * cores
     follows, leads = rank > 0, rank < group_size - 1
-    early = (z == 0) & follows
+    early = (z < 2) & follows
+    listens = (z == 0) & follows
     hub = (z == 0) & (c == 1)
     pair = x + 1 - 2 * (x % 2)
 
@@ -93,7 +94,7 @@
         pltpu.make_async_copy(weight_in, weight, local_sem.at[3]),
         pltpu.make_async_copy(bias_in, bias, local_sem.at[4]),
     ]
-    for copy in copies:
+    for copy in (copies[1], copies[0], copies[3], copies[4]):
         copy.start()
 
     @pl.when(leads)
@@ -104,19 +105,20 @@
     def _():
         tell(prv)
 
-    @pl.when(hub)
-    def _():
-        tell({"row_0": pair, "row_1": z, "row_2": c})
-        tell({"row_0": x, "row_1": z, "row_2": 0})
-        tell({"row_0": pair, "row_1": z, "row_2": 0})
-
+    @pl.when(listens)
+    def _():
         def spread(k, _):
-            for core in range(2):
-                tell({"row_0": x, "row_1": k, "row_2": core})
+            for core in range(cores):
+                there = (k == 0) & (core == c)
+
+                @pl.when(jnp.logical_not(there))
+                def _():
+                    tell({"row_0": x, "row_1": k, "row_2": core})
+
                 tell({"row_0": pair, "row_1": k, "row_2": core})
             return 0
 
-        lax.fori_loop(1, ring, spread, 0)
+        lax.fori_loop(0, ring, spread, 0)
 
     copies[0].wait()
     held = [mask[t // cols, t % cols] for t in range(tiles)]
@@ -259,19 +261,26 @@
 
     mine = counts.at[pl.ds(local, 1)]
 
-    def count_to(plane):
+    def count_to(plane, core):
         return pltpu.make_async_remote_copy(
             mine, mine, many_sem.at[0], many_sem.at[1],
-            device_id={"row_0": plane, "row_1": 0, "row_2": 1}, device_id_type=MESH,
+            device_id={"row_0": plane, "row_1": 0, "row_2": core}, device_id_type=MESH,
         )
 
+    hearers = [
+        (plane, core, (((plane > 0) | (core > 0)) & jnp.logical_not(here & (z == 0) & (c == core))))
+        for plane, here in ((x, True), (pair, False))
+        for core in range(2)
+    ]
+
     def arrive():
-        pl.semaphore_wait(barrier, 2 - hub.astype(I32) + follows.astype(I32) + leads.astype(I32))
-        count_to(pair).start()
-
-        @pl.when(jnp.logical_not(hub))
-        def _():
-            count_to(x).start()
+        others = sum((used.astype(I32) for _, _, used in hearers), jnp.int32(0))
+        pl.semaphore_wait(barrier, others + follows.astype(I32) + leads.astype(I32))
+        for plane, core, used in hearers:
+
+            @pl.when(used)
+            def _(plane=plane, core=core):
+                count_to(plane, core).start()
 
     note = remote(note_send, note_in, 0, nxt)
     down = remote(last_send, above_in, 1, nxt)
@@ -337,6 +346,7 @@
         arrive()
 
     copies[1].wait()
+    copies[2].start()
     stage(1)
     outer_row(last_row, last_send, rows_dev - 1, side - 16, 15)
 
@@ -393,29 +403,6 @@
 
     join(above, edge_first, 0, 0, 0, 0)
 
-    @pl.when(hub)
-    def _():
-        others = counts.at[pl.ds(0, 2 * ring * cores - 1)]
-        pltpu.make_async_copy(others, others, many_sem.at[1]).wait()
-        table = counts[...]
-        spot = lax.broadcasted_iota(I32, table.shape, 0) == lax.broadcasted_iota(I32, table.shape, 1)
-        line_send[...] = jnp.sum(jnp.where(spot, table, 0), axis=0, keepdims=True)
-
-        def line_to(k, core):
-            return pltpu.make_async_remote_copy(
-                line_send, line_in, many_sem.at[2], many_sem.at[3],
-                device_id={"row_0": x, "row_1": k, "row_2": core}, device_id_type=MESH,
-            )
-
-        line_to(0, 0).start()
-
-        def spread(k, _):
-            for core in range(2):
-                line_to(k, core).start()
-            return 0
-
-        lax.fori_loop(1, ring, spread, 0)
-
     def taken(a):
         came = jnp.max(note_in[a : a + 1, :])
         row, col = came // cols, came % cols
@@ -436,24 +423,57 @@
         note.wait_recv()
         fixed_rims.wait_recv()
         taken(1)
-        last_rim.wait_recv()
-        taken(0)
-
-    @pl.when(jnp.logical_not(hub))
+
+    @pl.when(listens)
+    def _():
+        others = counts.at[pl.ds(0, 2 * ring * cores - 1)]
+        pltpu.make_async_copy(others, others, many_sem.at[1]).wait()
+        table = counts[...]
+        spot = lax.broadcasted_iota(I32, table.shape, 0) == lax.broadcasted_iota(I32, table.shape, 1)
+        line_send[...] = jnp.sum(jnp.where(spot, table, 0), axis=0, keepdims=True)
+
+    @pl.when(hub)
+    def _():
+        def spread(k, _):
+            for core in range(2):
+                pltpu.make_async_remote_copy(
+                    line_send, line_in, many_sem.at[2], many_sem.at[3],
+                    device_id={"row_0": x, "row_1": k, "row_2": core}, device_id_type=MESH,
+                ).start()
+            return 0
+
+        lax.fori_loop(1, ring, spread, 0)
+
+    @pl.when(z > 0)
     def _():
         pltpu.make_async_copy(line_in, line_in, many_sem.at[3]).wait()
 
-    line = jnp.where(hub, line_send[...], line_in[...])
+    @pl.when(jnp.logical_not(follows))
+    def _():
+        line_in[...] = jnp.zeros(line_in.shape, I32)
+
+    line = jnp.where(listens, line_send[...], line_in[...])
     before = jnp.sum(jnp.where(lane < local, line, 0))
     whole = jnp.sum(line)
     start = jnp.where(x < planes // 2, 0, SLOTS * ring * cores * 2 - whole)
-    excess = start + before - SLOTS * local
-    excess = jnp.clip(excess, 0, SHIFT_MOST)
-    for j in range(SLOTS):
+    excess = jnp.clip(start + before - SLOTS * local, 0, SHIFT_MOST)
+
+    def fill(j):
         own = order[jnp.clip(j - excess, 0, SLOTS - 1)]
         came = tiles + SHIFT_MOST - excess + j
         out[j] = done[jnp.clip(jnp.where(j < excess, came, own), 0, tiles + SHIFT_MOST - 1)]
 
+    for j in range(SHIFT_MOST, SLOTS):
+        fill(j)
+
+    @pl.when(follows)
+    def _():
+        last_rim.wait_recv()
+        taken(0)
+
+    for j in range(SHIFT_MOST):
+        fill(j)
+
     @pl.when(leads)
     def _():
         for copy in (note, down, *bodies, fixed_rims, last_rim):
@@ -463,15 +483,15 @@
     def _():
         up.wait_send()
 
-    count_to(pair).wait_send()
-
-    @pl.when(jnp.logical_not(hub))
-    def _():
-        count_to(x).wait_send()
+    for plane, core, used in hearers:
+
+        @pl.when(used)
+        def _(plane=plane, core=core):
+            count_to(plane, core).wait_send()
 
     @pl.when(hub)
     def _():
-        sent = counts.at[pl.ds(0, ring * cores - 1)]
+        sent = counts.at[pl.ds(0, (ring - 1) * cores)]
         pltpu.make_async_copy(sent, sent, many_sem.at[2]).wait()
 
 

time: 31.5 us -> 30.3 us (0.962)
  the two profiles are of different devices: /device:TPU:160 before, /device:TPU:46 now
where the time goes in v3:
time: 30.3 us; the launch traced here: 30.1 us
  Pallas kernels  29.1 us (96%)
  local copies, waits for them, and re-layouts  0.97 us (3%)
    pallas_call x1, Pallas kernels, on_device(): pl.pallas_call(kernel, out_shape=pltpu.VMEM((SLOTS, side, width), BF16),...  29.1 us
    unnamed x1, local copies, waits for them, and re-layouts  0.97 us

profile of v3, /device:TPU:46, one launch (start us, length us, event | category | flops | bytes accessed | tf_op | source)
XLA Modules:
  0.0 30.1 jit_solution(11896640596016226820)
XLA Ops:
  0.0 29.1 %tissue_tiles.1 = bf16[8,32,2048]{2,1,0:T(8,128)(2,1)S(1)} custom-call(bf16[64,16384]{1,0:T(8,128)(2,1)} %pixels.1, s32[2,8]{1,0:T(2,128)} %mask_in.1, bf16[3,3,64,64]{3,2,1,0:T(8,128)(2,1)} %weight_in.1, bf16[64]{0:T(256)(128)(2,1)} %bias_in.1), custom_call_target="tpu_custom_call" | custom-call | tf_op jit(solution)/shard_map/tissue_tiles/pallas_call | solution.py:517
  29.1 1.0 %copy.6 = bf16[8,32,2048]{2,1,0:T(8,128)(2,1)} copy(bf16[8,32,2048]{2,1,0:T(8,128)(2,1)S(1)} %tissue_tiles.1) | data formatting | bytes 2097152

commit v4 on v3

--- a/solution.py
+++ b/solution.py
@@ -55,6 +55,7 @@
     line_send,
     line_in,
     order,
+    excess,
     local_sem,
     send_sem,
     recv_sem,
@@ -69,11 +70,13 @@
     groups = chunks // 2
     total = cols * chunks
     rank = (x * ring + z) * cores + c
+    local = (x % 2) * (ring * cores) + z * cores + c
     group_size = planes * ring * cores
     follows, leads = rank > 0, rank < group_size - 1
     early = (z < 2) & follows
-    listens = (z == 0) & follows
-    hub = (z == 0) & (c == 1)
+    hub = (z == 1) & (c == 1)
+    inner = x > 0
+    listens = (c == 1) & (z == 1 - inner.astype(I32))
     pair = x + 1 - 2 * (x % 2)
 
     def place(r):
@@ -89,12 +92,13 @@
     bands = (top_band, low_band)
     copies = [
         pltpu.make_async_copy(mask_in, mask, local_sem.at[0]),
-        pltpu.make_async_copy(pixels.at[side : 2 * side], low_band, local_sem.at[1]),
-        pltpu.make_async_copy(pixels.at[0:side], top_band, local_sem.at[2]),
-        pltpu.make_async_copy(weight_in, weight, local_sem.at[3]),
-        pltpu.make_async_copy(bias_in, bias, local_sem.at[4]),
+        pltpu.make_async_copy(pixels.at[side : 2 * side - 16], low_band.at[0 : side - 16], local_sem.at[2]),
+        pltpu.make_async_copy(pixels.at[0:side], top_band, local_sem.at[0]),
+        pltpu.make_async_copy(weight_in, weight, local_sem.at[1]),
+        pltpu.make_async_copy(bias_in, bias, local_sem.at[2]),
+        pltpu.make_async_copy(pixels.at[2 * side - 16 : 2 * side], low_band.at[side - 16 : side], local_sem.at[1]),
     ]
-    for copy in (copies[1], copies[0], copies[3], copies[4]):
+    for copy in (copies[0], copies[5], copies[1]):
         copy.start()
 
     @pl.when(leads)
@@ -109,7 +113,7 @@
     def _():
         def spread(k, _):
             for core in range(cores):
-                there = (k == 0) & (core == c)
+                there = (k == z) & (core == c)
 
                 @pl.when(jnp.logical_not(there))
                 def _():
@@ -122,21 +126,6 @@
 
     copies[0].wait()
     held = [mask[t // cols, t % cols] for t in range(tiles)]
-    upto = []
-    running = jnp.int32(0)
-    for t in range(tiles):
-        running = running + held[t]
-        upto.append(running)
-    own_count = running
-
-    def nth(k):
-        return sum(((upto[t] <= k).astype(I32) for t in range(tiles - 1)), jnp.int32(0))
-
-    local = (x % 2) * (ring * cores) + z * cores + c
-    counts[pl.ds(local, 1), :] = jnp.broadcast_to(own_count, (1, LANES))
-    sent_tiles = [nth(own_count - SHIFT_MOST + a) for a in range(SHIFT_MOST)]
-    for a in range(SHIFT_MOST):
-        note_send[a : a + 1, :] = jnp.broadcast_to(sent_tiles[a], (1, LANES))
     def keep(row, col):
         inside = (col >= 0) & (col < cols)
         return jnp.where(inside, mask[row, jnp.clip(col, 0, cols - 1)], 0).astype(F32)
@@ -166,10 +155,10 @@
             return low if a else jnp.where(row == 0, top_band[:, lanes_of(col, k)], low)
 
         for k in range(chunks):
-            tile_send[a, k] = pixels_of(k)
+            tile_send[a, k + 1] = pixels_of(k)
         right = pixels_of(chunks).astype(F32) * keep(row, col + 1)
         left = pixels_of(-1).astype(F32) * keep(row, col - 1)
-        tile_send[a, chunks] = jnp.where(lower, right, left).astype(BF16)
+        tile_send[a, 0] = jnp.where(lower, right, left).astype(BF16)
 
     def one(source, pick):
         return source.astype(F32)[pick : pick + 1, :]
@@ -206,21 +195,23 @@
         short = bias[...].astype(F32).reshape(1, 64)
         return jnp.concatenate([short] * 4, axis=1)
 
-    def multiply():
+    def multiply(first=0, last=groups):
         for dy in range(3):
             rows = slice(7 + dy, 7 + dy + side)
-            for g in range(groups):
-                at = slice(g * side, (g + 1) * side)
+            for g in range(first, last):
+                at = slice((g - first) * side, (g - first + 1) * side)
                 right = fat[2 * g + 2 if g < groups - 1 else chunks, rows, :]
                 left = fat[2 * g - 1 if g > 0 else chunks, rows, :]
                 lhs[at, dy * 384 : dy * 384 + 128] = fat[2 * g, rows, :].astype(BF16)
                 lhs[at, dy * 384 + 128 : dy * 384 + 256] = fat[2 * g + 1, rows, :].astype(BF16)
                 lhs[at, dy * 384 + 256 : dy * 384 + 384] = jnp.where(lower, right, left).astype(BF16)
-        return jnp.dot(lhs[...], big[...], preferred_element_type=F32) + bias_row()
-
-    def finish(result, slot):
-        for g in range(groups):
-            done[slot, :, g * 256 : (g + 1) * 256] = result[g * side : (g + 1) * side].astype(BF16)
+        used = lhs[0 : (last - first) * side]
+        return jnp.dot(used, big[...], preferred_element_type=F32) + bias_row()
+
+    def finish(result, slot, first=0, last=groups):
+        for g in range(first, last):
+            part = result[(g - first) * side : (g - first + 1) * side]
+            done[slot, :, g * 256 : (g + 1) * 256] = part.astype(BF16)
 
     def own_tiles():
         build_big()
@@ -254,68 +245,92 @@
 
             lax.fori_loop(0, cols, tile, 0)
 
-    def remote(source, target, k, where):
+    def remote(source, target, sent, came, where):
         return pltpu.make_async_remote_copy(
-            source, target, send_sem.at[k], recv_sem.at[k], device_id=where, device_id_type=MESH
+            source, target, send_sem.at[sent], recv_sem.at[came], device_id=where, device_id_type=MESH
         )
 
     mine = counts.at[pl.ds(local, 1)]
 
-    def count_to(plane, core):
+    def count_to(plane):
+        level = 1 - (plane > 0).astype(I32)
         return pltpu.make_async_remote_copy(
             mine, mine, many_sem.at[0], many_sem.at[1],
-            device_id={"row_0": plane, "row_1": 0, "row_2": core}, device_id_type=MESH,
+            device_id={"row_0": plane, "row_1": level, "row_2": 1}, device_id_type=MESH,
         )
 
-    hearers = [
-        (plane, core, (((plane > 0) | (core > 0)) & jnp.logical_not(here & (z == 0) & (c == core))))
-        for plane, here in ((x, True), (pair, False))
-        for core in range(2)
+    hearers = [(x, jnp.logical_not(listens)), (pair, listens | jnp.logical_not(listens))]
+
+    def arrive():
+        others = 2 - listens.astype(I32)
+        pl.semaphore_wait(barrier, others + follows.astype(I32) + leads.astype(I32))
+
+    def send_counts():
+        for spot, used in hearers:
+
+            @pl.when(used)
+            def _(spot=spot):
+                count_to(spot).start()
+
+    note = remote(note_send, note_in, 0, 0, nxt)
+    down = remote(last_send, above_in, 1, 1, nxt)
+    up = remote(first_send, below_in, 2, 2, prv)
+    cut = chunks // 2 + 2
+    pieces = ((slice(0, cut), slice(cut, chunks + 1)), (slice(0, chunks + 1),))
+    bodies = [
+        [remote(tile_send.at[a, piece], tile_in.at[a, piece], 3, 4 + i - a, nxt) for i, piece in enumerate(pieces[a])]
+        for a in range(SHIFT_MOST)
     ]
-
-    def arrive():
-        others = sum((used.astype(I32) for _, _, used in hearers), jnp.int32(0))
-        pl.semaphore_wait(barrier, others + follows.astype(I32) + leads.astype(I32))
-        for plane, core, used in hearers:
-
-            @pl.when(used)
-            def _(plane=plane, core=core):
-                count_to(plane, core).start()
-
-    note = remote(note_send, note_in, 0, nxt)
-    down = remote(last_send, above_in, 1, nxt)
-    up = remote(first_send, below_in, 2, prv)
-    bodies = [remote(tile_send.at[a], tile_in.at[a], 3 + a, nxt) for a in range(SHIFT_MOST)]
-    fixed_rims = remote(rim_send.at[0:2], rim_in.at[0:2], 5, nxt)
-    last_rim = remote(rim_send.at[2], rim_in.at[2], 6, nxt)
+    rims = remote(rim_send, rim_in, 4, 6, nxt)
+
+    def send_halo():
+        @pl.when(leads)
+        def _():
+            down.start()
+
+    def low_tile():
+        copies[1].wait()
+        for copy in copies[2:5]:
+            copy.start()
+        stage(1)
+
     def send_low():
         @pl.when(leads)
         def _():
             note.start()
-            bodies[1].start()
-            down.start()
+            bodies[1][0].start()
 
     def send_top():
         stage(0)
         inner_rims()
 
+        @pl.when(jnp.logical_not(early))
+        def _():
+            send_last_rim()
+
         @pl.when(leads)
         def _():
-            fixed_rims.start()
-            bodies[0].start()
+            bodies[0][0].start()
+            bodies[0][1].start()
 
         outer_row(first_row, first_send, 0, 0, 0)
 
         @pl.when(follows)
         def _():
             up.start()
+
+    def rim_row(rim, k):
+        return rim * chunks + k if k < chunks else 3 * chunks + rim
+
+    def set_rim(rim, k, line):
+        at = rim_row(rim, k)
+        rim_work[at : at + 1, :] = line
 
     def inner_rims():
         for k, line in enumerate(inner_rim(1, 0, 0, sent_tiles[0] % cols)):
-            rim_work[0, k : k + 1, :] = line
+            set_rim(0, k, line)
         for k, line in enumerate(inner_rim(0, 15, side - 16, sent_tiles[1] % cols)):
-            rim_work[1, k : k + 1, :] = line
-        rim_send[0:2] = rim_work[0:2].astype(BF16)
+            set_rim(1, k, line)
 
     def send_last_rim():
         @pl.when(follows)
@@ -329,41 +344,59 @@
 
         row, col = sent_tiles[0] // cols, sent_tiles[0] % cols
         for k, (outer, inner) in enumerate(zip(edge_rim(above, col), inner_rim(0, 15, side - 16, col))):
-            rim_work[2, k : k + 1, :] = jnp.where(row == 0, outer, inner)
-        rim_send[2] = rim_work[2].astype(BF16)
+            set_rim(2, k, jnp.where(row == 0, outer, inner))
+        rim_send[...] = rim_work[...].astype(BF16)
 
         @pl.when(leads)
         def _():
-            last_rim.start()
-
+            rims.start()
+
+    copies[5].wait()
+    outer_row(last_row, last_send, rows_dev - 1, side - 16, 15)
+
+    @pl.when(jnp.logical_not(early))
+    def _():
+        arrive()
+        send_halo()
+
+    upto = []
+    running = jnp.int32(0)
+    for t in range(tiles):
+        running = running + held[t]
+        upto.append(running)
+    own_count = running
+
+    def nth(k):
+        return sum(((upto[t] <= k).astype(I32) for t in range(tiles - 1)), jnp.int32(0))
+
+    counts[pl.ds(local, 1), :] = jnp.broadcast_to(own_count, (1, LANES))
+    sent_tiles = [nth(own_count - SHIFT_MOST + a) for a in range(SHIFT_MOST)]
+    for a in range(SHIFT_MOST):
+        note_send[a : a + 1, :] = jnp.broadcast_to(sent_tiles[a], (1, LANES))
+    note_send[SHIFT_MOST : SHIFT_MOST + 1, :] = jnp.broadcast_to(own_count, (1, LANES))
     zeros8 = jnp.zeros((8, LANES), F32)
-    for ref in (first_row, last_row, above, below):
+    for ref in (first_row, above, below):
         ref[0:8, :] = zeros8
         ref[8 + total : 16 + total, :] = zeros8
 
-    @pl.when(jnp.logical_not(early))
-    def _():
-        arrive()
-
-    copies[1].wait()
-    copies[2].start()
-    stage(1)
-    outer_row(last_row, last_send, rows_dev - 1, side - 16, 15)
-
     @pl.when(early)
     def _():
+        low_tile()
         copies[2].wait()
         own_tiles()
         arrive()
+        send_counts()
+        send_halo()
         send_low()
         send_top()
 
     @pl.when(jnp.logical_not(early))
     def _():
+        send_counts()
+        low_tile()
         send_low()
         copies[2].wait()
         send_top()
-        send_last_rim()
         own_tiles()
 
     for k in range(SLOTS):
@@ -406,23 +439,60 @@
     def taken(a):
         came = jnp.max(note_in[a : a + 1, :])
         row, col = came // cols, came % cols
-        bodies[a].wait_recv()
-        for k in range(chunks + 1):
-            fat[k, 8 : 8 + side, :] = tile_in[a, k].astype(F32)
-        over = rim_in[1 if a else 2].astype(F32)
-        under = rim_in[0].astype(F32)
+        came_rims = rim_in[...].astype(F32)
+
+        def rim(which, k):
+            at = rim_row(which, k)
+            return came_rims[at : at + 1, :]
+
         for k, line in enumerate(edge_rim(first_row, col)):
-            fat[k, 7:8, :] = over[k : k + 1, :]
+            fat[k, 7:8, :] = rim(1 if a else 2, k)
             if a == 0:
-                line = jnp.where(row == rows_dev - 1, line, under[k : k + 1, :])
+                line = jnp.where(row == rows_dev - 1, line, rim(0, k))
             fat[k, 8 + side : 9 + side, :] = line
-        finish(multiply(), tiles + a)
+        for i, piece in enumerate(pieces[a]):
+            bodies[a][i].wait_recv()
+            for k in range(piece.start, piece.stop):
+                fat[k - 1 if k else chunks, 8 : 8 + side, :] = tile_in[a, k].astype(F32)
+            parts = len(pieces[a])
+            span = (i * groups // parts, (i + 1) * groups // parts)
+            result = multiply(*span)
+            if a:
+                finish(result, tiles, *span)
+            else:
+                lead_slot(result, *span)
+
+    def lead_slot(result, first, last):
+        for g in range(first, last):
+            part = result[(g - first) * side : (g - first + 1) * side].astype(BF16)
+            lanes = slice(g * 256, (g + 1) * 256)
+            out[0, :, lanes] = jnp.where(excess[0] == SHIFT_MOST, part, out[0, :, lanes])
+
+    @pl.when(leads)
+    def _():
+        for copy in (note, down, rims):
+            copy.wait_send()
+        pltpu.make_async_copy(tile_send, tile_send, send_sem.at[3]).wait()
 
     @pl.when(follows)
     def _():
+        up.wait_send()
+
+    for spot, used in hearers:
+
+        @pl.when(used)
+        def _(spot=spot):
+            count_to(spot).wait_send()
+
+    def settle(line):
+        before = jnp.sum(jnp.where(lane < local, line, 0))
+        whole = jnp.sum(line)
+        start = jnp.where(x < planes // 2, 0, SLOTS * ring * cores * 2 - whole)
+        excess[0] = jnp.clip(start + before - SLOTS * local, 0, SHIFT_MOST)
+
+    @pl.when(follows)
+    def _():
         note.wait_recv()
-        fixed_rims.wait_recv()
-        taken(1)
 
     @pl.when(listens)
     def _():
@@ -430,69 +500,80 @@
         pltpu.make_async_copy(others, others, many_sem.at[1]).wait()
         table = counts[...]
         spot = lax.broadcasted_iota(I32, table.shape, 0) == lax.broadcasted_iota(I32, table.shape, 1)
-        line_send[...] = jnp.sum(jnp.where(spot, table, 0), axis=0, keepdims=True)
+        line = jnp.sum(jnp.where(spot, table, 0), axis=0, keepdims=True)
+        line_send[...] = line
+        settle(line)
+
+    def line_to(source, level, core):
+        return pltpu.make_async_remote_copy(
+            source, line_in, many_sem.at[0], many_sem.at[2],
+            device_id={"row_0": x, "row_1": level, "row_2": core}, device_id_type=MESH,
+        )
+
+    @pl.when(listens & inner)
+    def _():
+        line_to(line_send, 0, 0).start()
+        line_to(line_send, 1, 1).start()
+
+    @pl.when(hub & jnp.logical_not(inner))
+    def _():
+        line_in[...] = line_send[...]
+
+    def hear():
+        pltpu.make_async_copy(line_in, line_in, many_sem.at[2]).wait()
+        settle(line_in[...])
+
+    @pl.when((z == 0) & (c == 0) & inner)
+    def _():
+        hear()
+
+    @pl.when(follows)
+    def _():
+        rims.wait_recv()
+        taken(1)
+
+    @pl.when((z > 0) & (inner | jnp.logical_not(hub)))
+    def _():
+        hear()
 
     @pl.when(hub)
     def _():
         def spread(k, _):
             for core in range(2):
-                pltpu.make_async_remote_copy(
-                    line_send, line_in, many_sem.at[2], many_sem.at[3],
-                    device_id={"row_0": x, "row_1": k, "row_2": core}, device_id_type=MESH,
-                ).start()
+                line_to(line_in, k, core).start()
             return 0
 
-        lax.fori_loop(1, ring, spread, 0)
-
-    @pl.when(z > 0)
-    def _():
-        pltpu.make_async_copy(line_in, line_in, many_sem.at[3]).wait()
-
-    @pl.when(jnp.logical_not(follows))
-    def _():
-        line_in[...] = jnp.zeros(line_in.shape, I32)
-
-    line = jnp.where(listens, line_send[...], line_in[...])
-    before = jnp.sum(jnp.where(lane < local, line, 0))
-    whole = jnp.sum(line)
-    start = jnp.where(x < planes // 2, 0, SLOTS * ring * cores * 2 - whole)
-    excess = jnp.clip(start + before - SLOTS * local, 0, SHIFT_MOST)
-
-    def fill(j):
-        own = order[jnp.clip(j - excess, 0, SLOTS - 1)]
-        came = tiles + SHIFT_MOST - excess + j
-        out[j] = done[jnp.clip(jnp.where(j < excess, came, own), 0, tiles + SHIFT_MOST - 1)]
-
-    for j in range(SHIFT_MOST, SLOTS):
-        fill(j)
+        line_to(line_in, 1, 0).start()
+        lax.fori_loop(2, ring, spread, 0)
+
+    @pl.when(rank == 0)
+    def _():
+        excess[0] = jnp.int32(0)
+
+    @pl.when(rank == 1)
+    def _():
+        beside = jnp.max(note_in[SHIFT_MOST : SHIFT_MOST + 1, :])
+        excess[0] = jnp.clip(beside - SLOTS, 0, SHIFT_MOST)
+
+    shift = excess[0]
+
+    for j in range(SLOTS):
+        own = order[jnp.clip(j - shift, 0, SLOTS - 1)]
+        out[j] = done[jnp.where(j == shift - 1, tiles, own)]
 
     @pl.when(follows)
     def _():
-        last_rim.wait_recv()
         taken(0)
 
-    for j in range(SHIFT_MOST):
-        fill(j)
-
-    @pl.when(leads)
-    def _():
-        for copy in (note, down, *bodies, fixed_rims, last_rim):
-            copy.wait_send()
-
-    @pl.when(follows)
-    def _():
-        up.wait_send()
-
-    for plane, core, used in hearers:
-
-        @pl.when(used)
-        def _(plane=plane, core=core):
-            count_to(plane, core).wait_send()
+    @pl.when(listens & inner)
+    def _():
+        both = counts.at[pl.ds(0, 2)]
+        pltpu.make_async_copy(both, both, many_sem.at[0]).wait()
 
     @pl.when(hub)
     def _():
-        sent = counts.at[pl.ds(0, (ring - 1) * cores)]
-        pltpu.make_async_copy(sent, sent, many_sem.at[2]).wait()
+        sent = counts.at[pl.ds(0, (ring - 1) * cores - 1)]
+        pltpu.make_async_copy(sent, sent, many_sem.at[0]).wait()
 
 
 def in_hbm(array):
@@ -511,7 +592,7 @@
     half = pltpu.VMEM((side, slide_pixels.shape[1]), BF16)
     strip = pltpu.VMEM((total + 16, LANES), F32)
     packed = pltpu.VMEM((total, LANES), BF16)
-    rim = pltpu.VMEM((3, 32, LANES), BF16)
+    rim = pltpu.VMEM((4 * chunks, LANES), BF16)
     tile_pair = pltpu.VMEM((SHIFT_MOST, chunks + 1, side, LANES), BF16)
     edge = pltpu.VMEM((cols, groups, 256), F32)
     return pl.pallas_call(
@@ -528,7 +609,7 @@
             pltpu.VMEM((3 * 384, 256), BF16),
             pltpu.VMEM((chunks + 1, 48, LANES), F32),
             pltpu.VMEM((groups * side, 3 * 384), BF16),
-            pltpu.VMEM((tiles + SHIFT_MOST, side, width), BF16),
+            pltpu.VMEM((tiles + 1, side, width), BF16),
             edge,
             edge,
             strip,
@@ -541,19 +622,20 @@
             strip,
             tile_pair,
             tile_pair,
-            pltpu.VMEM((3, 32, LANES), F32),
+            pltpu.VMEM((4 * chunks, LANES), F32),
             rim,
             rim,
-            pltpu.VMEM((SHIFT_MOST, LANES), I32),
-            pltpu.VMEM((SHIFT_MOST, LANES), I32),
+            pltpu.VMEM((SHIFT_MOST + 1, LANES), I32),
+            pltpu.VMEM((SHIFT_MOST + 1, LANES), I32),
             pltpu.VMEM((pair_size, LANES), I32),
             pltpu.VMEM((1, LANES), I32),
             pltpu.VMEM((1, LANES), I32),
             pltpu.SMEM((SLOTS,), I32),
+            pltpu.SMEM((1,), I32),
+            pltpu.SemaphoreType.DMA((3,)),
             pltpu.SemaphoreType.DMA((5,)),
             pltpu.SemaphoreType.DMA((7,)),
-            pltpu.SemaphoreType.DMA((7,)),
-            pltpu.SemaphoreType.DMA((4,)),
+            pltpu.SemaphoreType.DMA((3,)),
         ],
         compiler_params=pltpu.CompilerParams(
             collective_id=0, has_side_effects=True, vmem_limit_bytes=24 * 1024 * 1024

time: 30.3 us -> 29.8 us (0.983)
  Pallas kernels: 29.1 us -> 28.5 us
    pallas_call x1, Pallas kernels: 29.1 us -> 28.5 us  [on_device(): pl.pallas_call(kernel, out_shape=pltpu.VMEM((SLOTS, side, width), BF16),...]
where the time goes in v4:
time: 29.8 us; the launch traced here: 29.5 us
  Pallas kernels  28.5 us (96%)
  local copies, waits for them, and re-layouts  0.97 us (3%)
    pallas_call x1, Pallas kernels, on_device(): pl.pallas_call(kernel, out_shape=pltpu.VMEM((SLOTS, side, width), BF16),...  28.5 us
    unnamed x1, local copies, waits for them, and re-layouts  0.97 us

profile of v4, /device:TPU:46, one launch (start us, length us, event | category | flops | bytes accessed | tf_op | source)
XLA Modules:
  0.0 29.5 jit_solution(6510869637313235050)
XLA Ops:
  0.0 28.5 %tissue_tiles.1 = bf16[8,32,2048]{2,1,0:T(8,128)(2,1)S(1)} custom-call(bf16[64,16384]{1,0:T(8,128)(2,1)} %pixels.1, s32[2,8]{1,0:T(2,128)} %mask_in.1, bf16[3,3,64,64]{3,2,1,0:T(8,128)(2,1)} %weight_in.1, bf16[64]{0:T(256)(128)(2,1)} %bias_in.1), custom_call_target="tpu_custom_call" | custom-call | tf_op jit(solution)/shard_map/tissue_tiles/pallas_call | solution.py:598
  28.5 1.0 %copy.6 = bf16[8,32,2048]{2,1,0:T(8,128)(2,1)} copy(bf16[8,32,2048]{2,1,0:T(8,128)(2,1)S(1)} %tissue_tiles.1) | data formatting | bytes 2097152

commit v5 on v4

--- a/solution.py
+++ b/solution.py
@@ -485,10 +485,11 @@
             count_to(spot).wait_send()
 
     def settle(line):
-        before = jnp.sum(jnp.where(lane < local, line, 0))
-        whole = jnp.sum(line)
-        start = jnp.where(x < planes // 2, 0, SLOTS * ring * cores * 2 - whole)
-        excess[0] = jnp.clip(start + before - SLOTS * local, 0, SHIFT_MOST)
+        first_half = x < planes // 2
+        side_wanted = (lane < local) == first_half
+        part = jnp.sum(jnp.where(side_wanted & (lane < 2 * ring * cores), line, 0))
+        before = jnp.where(first_half, part, SLOTS * 2 * ring * cores - part)
+        excess[0] = jnp.clip(before - SLOTS * local, 0, SHIFT_MOST)
 
     @pl.when(follows)
     def _():
@@ -523,16 +524,12 @@
         pltpu.make_async_copy(line_in, line_in, many_sem.at[2]).wait()
         settle(line_in[...])
 
-    @pl.when((z == 0) & (c == 0) & inner)
-    def _():
-        hear()
-
     @pl.when(follows)
     def _():
         rims.wait_recv()
         taken(1)
 
-    @pl.when((z > 0) & (inner | jnp.logical_not(hub)))
+    @pl.when((inner | (z > 0)) & jnp.logical_not(listens))
     def _():
         hear()
 

time: 29.8 us -> 29.6 us (level)
  no operation moved by 1% of the time
where the time goes in v5:
time: 29.6 us; the launch traced here: 29.5 us
  Pallas kernels  28.5 us (96%)
  local copies, waits for them, and re-layouts  0.97 us (3%)
    pallas_call x1, Pallas kernels, on_device(): pl.pallas_call(kernel, out_shape=pltpu.VMEM((SLOTS, side, width), BF16),...  28.5 us
    unnamed x1, local copies, waits for them, and re-layouts  0.97 us

profile of v5, /device:TPU:46, one launch (start us, length us, event | category | flops | bytes accessed | tf_op | source)
XLA Modules:
  0.0 29.5 jit_solution(11752544863430217551)
XLA Ops:
  0.0 28.5 %tissue_tiles.1 = bf16[8,32,2048]{2,1,0:T(8,128)(2,1)S(1)} custom-call(bf16[64,16384]{1,0:T(8,128)(2,1)} %pixels.1, s32[2,8]{1,0:T(2,128)} %mask_in.1, bf16[3,3,64,64]{3,2,1,0:T(8,128)(2,1)} %weight_in.1, bf16[64]{0:T(256)(128)(2,1)} %bias_in.1), custom_call_target="tpu_custom_call" | custom-call | tf_op jit(solution)/shard_map/tissue_tiles/pallas_call | solution.py:595
  28.5 1.0 %copy.6 = bf16[8,32,2048]{2,1,0:T(8,128)(2,1)} copy(bf16[8,32,2048]{2,1,0:T(8,128)(2,1)S(1)} %tissue_tiles.1) | data formatting | bytes 2097152
